TPU v7x, 32 devices: a whole 2x2x4 slice. The times are simulated.
32 devices in a mesh: grp: 2 (over core), dev: 16 (over z, y, x).
Axes of the slice: x: 2, y: 2, z: 4, core: 2. Of those that a mesh axis runs over, the one named last changes fastest.
Arguments:
- user_factors: float32 [4096, 256], P(('grp', 'dev')), may hold values from -0.5 to 0.5
- item_factors: float32 [2048, 256], P(('grp', 'dev')), may hold values from -0.5 to 0.5
- user_items: int32 [4096, 2, 3], P(('grp', 'dev')), may hold values from 0 to 1023, as said below
- user_conf: float32 [4096, 2, 3], P(('grp', 'dev')), may hold values from 1 to 200
- user_mask: int32 [4096, 2, 3], P(('grp', 'dev')), may hold values 0 or 1
- item_users: int32 [2048, 2, 6], P(('grp', 'dev')), may hold values from 0 to 2047, as said below
- item_conf: float32 [2048, 2, 6], P(('grp', 'dev')), may hold values from 1 to 200
- item_mask: int32 [2048, 2, 6], P(('grp', 'dev')), may hold values 0 or 1
Outputs:
- new_users: float32 [4096, 256], P(('grp', 'dev'))
- new_items: float32 [2048, 256], P(('grp', 'dev'))
Inputs may be any that keep to these rules, and one draw needn't show every extreme that they name: Within owner block c, id // 64 is the owner device and id % 64 its row. The user_items of the users of one device, in one owner block, name at most 16 distinct rows of any one owner device, and in every block each device names exactly 16 distinct rows of some owner device. Within owner block c, id // 128 is the owner device and id % 128 its row. The item_users of the items of one device, in one owner block, name at most 16 distinct rows of any one owner device, and in every block each device names exactly 16 distinct rows of some owner device.
All inputs are finite; a program needn't handle non-finite values. No bound on the sum of `user_mask` or of `item_mask` on one device may be relied on, other than what follows from the above.
Results may differ from a plain program's by a relative error of at most 0.0044.
Values may be sent and summed in bfloat16 or wider, within the bound.
No kernel may reach another device: no remote copies, remote signals or barrier semaphores. Data moves between devices by JAX's collectives and lax.ppermute only.
A program may use at most 128 MiB of HBM per device.

v0:
```python
import jax
import jax.numpy as jnp
from jax import lax
from jax.sharding import PartitionSpec as P

CG_STEPS = 4


ridge = 1.0


def solve_rows(gram, start_x, rows, confidence, slot_mask):
    maskf = slot_mask.astype(jnp.float32)
    weight = confidence * maskf
    rhs = jnp.einsum(
        "us,usr->ur", maskf * (1.0 + confidence), rows, precision=lax.Precision.HIGHEST
    )

    def apply(vector):
        along = jnp.einsum("usr,ur->us", rows, vector, precision=lax.Precision.HIGHEST)
        extra = jnp.einsum("us,usr->ur", weight * along, rows, precision=lax.Precision.HIGHEST)
        return jnp.dot(vector, gram, precision=lax.Precision.HIGHEST) + ridge * vector + extra

    solution = start_x
    resid = rhs - apply(solution)
    direction = resid
    norm_now = jnp.sum(resid * resid, axis=1, keepdims=True)
    for step in range(CG_STEPS):
        image = apply(direction)
        alpha = norm_now / jnp.sum(direction * image, axis=1, keepdims=True)
        solution = solution + alpha * direction
        resid = resid - alpha * image
        norm_next = jnp.sum(resid * resid, axis=1, keepdims=True)
        direction = resid + norm_next / norm_now * direction
        norm_now = norm_next
    return solution


def gram_of(block):
    return lax.dot_general(
        block, block, (((0,), (0,)), ((), ())), preferred_element_type=jnp.float32
    )


def collect(whole, row_index, mask_now):
    picked = jnp.take(whole, row_index, axis=0).astype(jnp.float32)
    return picked * mask_now[..., None].astype(jnp.float32)


def half_step(start_x, other, slot_ids, confidence, slot_mask):
    local_rows = other.shape[0]
    groups = lax.axis_size("grp")
    packed = other.astype(jnp.bfloat16)
    row_parts = []
    conf_parts = []
    mask_parts = []
    stacked = lax.all_gather(packed, "grp", axis=0, tiled=True)
    whole = lax.all_gather(stacked, "dev", axis=0, tiled=True)
    for span in range(groups):
        local = slot_ids[:, span, :]
        row_index = (
            local // local_rows * (groups * local_rows) + span * local_rows + local % local_rows
        )
        row_parts.append(collect(whole, row_index, slot_mask[:, span, :]))
        conf_parts.append(confidence[:, span, :])
        mask_parts.append(slot_mask[:, span, :])
    squares = gram_of(whole)
    rows = jnp.concatenate(row_parts, axis=1)
    conf_all = jnp.concatenate(conf_parts, axis=1)
    mask_all = jnp.concatenate(mask_parts, axis=1)
    return solve_rows(squares, start_x, rows, conf_all, mask_all)


def per_device(
    user_factors, item_factors, user_items, user_conf, user_mask, item_users, item_conf, item_mask
):
    new_users = half_step(user_factors, item_factors, user_items, user_conf, user_mask)
    new_items = half_step(item_factors, new_users, item_users, item_conf, item_mask)
    return (new_users, new_items)


def solution(mesh):
    return jax.shard_map(
        per_device,
        mesh=mesh,
        in_specs=(
            P(("grp", "dev"), None),
            P(("grp", "dev"), None),
            P(("grp", "dev"), None, None),
            P(("grp", "dev"), None, None),
            P(("grp", "dev"), None, None),
            P(("grp", "dev"), None, None),
            P(("grp", "dev"), None, None),
            P(("grp", "dev"), None, None),
        ),
        out_specs=(P(("grp", "dev"), None), P(("grp", "dev"), None)),
        check_vma=False,
    )
```

profile of v0, /device:TPU:0, one launch (start us, length us, event | category | flops | bytes accessed | tf_op | source)
XLA Modules:
  0.0 183.1 jit_solution(7318223275337007438)
XLA Ops:
  7.2 0.8 convert_element_type.57
  8.1 2.1 %all_gather.12 = bf16[128,256]{1,0:T(8,128)(2,1)} all-gather(bf16[64,256]{1,0:T(8,128)(2,1)S(1)} %convert_element_type.57), channel_id=1, replica_groups=mesh['grp'=2,'dev'=16] {'grp'}, dimensions={0}, use_global_device_ids=true | all-gather | bytes 98304 | tf_op jit(solution)/shard_map/all_gather | solution.py:57
  10.2 0.8 fusion.85
  11.1 0.2 reshape.170
  11.4 0.8 fusion.84
  12.2 0.1 copy.42
  12.5 0.2 reshape.166
  12.8 0.1 copy.39
  13.0 1.0 copy.47
  14.0 0.8 fusion.83
  14.8 53.8 %all-gather.3.cloned.1.call-done = bf16[2048,256]{1,0:T(8,128)(2,1)} async-done(((bf16[128,256]{1,0:T(8,128)(2,1)}), bf16[2048,256]{1,0:T(8,128)(2,1)}) %all-gather.3.cloned.1.call-update) | async-done | bytes 1048592 | tf_op jit(solution)/shard_map/all_gather | solution.py:58
  68.6 3.1 %gather_fusion.1 = bf16[384,256]{1,0:T(8,128)(2,1)S(1)} fusion(bf16[2048,256]{1,0:T(8,128)(2,1)} %all-gather.3.cloned.1.call-done, s32[1024]{0:T(1024)S(1)} %pad_clamp_fusion.2), kind=kCustom, calls=%fused_computation.2.clone | custom fusion | bytes 394752 | tf_op jit(solution)/shard_map/jit(_take)/gather | solution.py:46
  71.8 2.2 %gather_fusion = bf16[384,256]{1,0:T(8,128)(2,1)S(1)} fusion(bf16[2048,256]{1,0:T(8,128)(2,1)S(1)} %copy-done, s32[1024]{0:T(1024)S(1)} %pad_clamp_fusion.3), kind=kCustom, calls=%fused_computation.clone | custom fusion | bytes 394752 | tf_op jit(solution)/shard_map/jit(_take)/gather | solution.py:46
  74.2 0.3 convert_multiply_fusion.2
  74.5 0.3 convert_multiply_fusion.3
  74.9 1.3 fusion.18
  76.5 0.8 multiply_reduce_fusion.8
  77.5 0.5 fusion.86
  78.0 0.6 fusion.7
  78.7 0.4 multiply_reduce_fusion.7
  79.1 0.1 copy.160
  79.3 0.5 multiply_reduce_fusion.6
  79.9 0.6 multiply_reduce_fusion.15
  80.7 0.4 multiply_reduce_fusion.5
  81.3 0.5 multiply_reduce_fusion.4
  81.9 0.6 multiply_reduce_fusion.13
  82.7 0.4 multiply_reduce_fusion.3
  83.1 0.1 copy.174
  83.3 0.5 multiply_reduce_fusion.2
  83.9 0.6 multiply_reduce_fusion.11
  84.7 0.4 multiply_reduce_fusion.1
  85.3 0.5 multiply_reduce_fusion
  85.9 0.6 fusion.8
  86.6 2.1 %all_gather.14 = bf16[256,256]{0,1:T(8,128)(2,1)} all-gather(bf16[128,256]{0,1:T(8,128)(2,1)S(1)} %get-tuple-element.22), channel_id=1, replica_groups=mesh['grp'=2,'dev'=16] {'grp'}, dimensions={0}, use_global_device_ids=true | all-gather | bytes 196608 | tf_op jit(solution)/shard_map/all_gather | solution.py:57
  88.9 0.1 reshape.178
  89.4 0.1 reshape.174
  89.8 0.8 copy.65
  90.5 61.9 %all-gather.5.cloned.1.call-done = bf16[4096,256]{0,1:T(8,128)(2,1)} async-done(((bf16[256,256]{0,1:T(8,128)(2,1)}), bf16[4096,256]{0,1:T(8,128)(2,1)}) %all-gather.5.cloned.1.call-update) | async-done | bytes 2097168 | tf_op jit(solution)/shard_map/all_gather | solution.py:58
  152.4 3.3 %copy.58 = bf16[4096,256]{1,0:T(8,128)(2,1)S(1)} copy(bf16[4096,256]{0,1:T(8,128)(2,1)} %all-gather.5.cloned.1.call-done) | data formatting | bytes 4194304 | tf_op jit(solution)/shard_map/all_gather | solution.py:58
  155.7 2.1 %gather_fusion.3 = bf16[384,256]{1,0:T(8,128)(2,1)S(1)} fusion(bf16[4096,256]{1,0:T(8,128)(2,1)S(1)} %copy.58, s32[1024]{0:T(1024)S(1)} %pad_clamp_fusion), kind=kCustom, calls=%fused_computation.3.clone | custom fusion | bytes 394752 | tf_op jit(solution)/shard_map/jit(_take)/gather | solution.py:46
  157.9 2.3 %gather_fusion.2 = bf16[384,256]{1,0:T(8,128)(2,1)S(1)} fusion(bf16[4096,256]{1,0:T(8,128)(2,1)S(1)} %copy.58, s32[1024]{0:T(1024)S(1)} %pad_clamp_fusion.1), kind=kCustom, calls=%fused_computation.1.clone | custom fusion | bytes 394752 | tf_op jit(solution)/shard_map/jit(_take)/gather | solution.py:46
  160.2 0.2 convert_multiply_fusion
  160.4 0.2 convert_multiply_fusion.1
  160.7 1.1 fusion.28
  162.0 0.8 fusion.75
  162.9 0.8 fusion.76
  163.7 0.7 fusion.87
  164.4 0.3 fusion.11
  164.7 1.1 fusion.26
  166.0 0.8 fusion.74
  166.8 0.3 multiply_reduce_fusion.22
  167.2 0.2 multiply_reduce_fusion.21
  167.5 1.1 fusion.24
  168.8 0.8 fusion.73
  169.6 0.3 multiply_reduce_fusion.20
  169.9 0.2 multiply_reduce_fusion.19
  170.2 1.1 fusion.22
  171.6 0.8 fusion.72
  172.4 0.3 multiply_reduce_fusion.18
  172.7 0.2 multiply_reduce_fusion.17
  173.0 1.1 fusion.20
  174.3 0.8 fusion.71
  175.1 0.3 fusion.17
  175.5 0.7 multiply_add_fusion.4
  (109 shorter events, 5.1 us)
Async XLA Ops:
  7.2 61.4 %all-gather.3.cloned.1.call-start = ((), (), s32[]{:S(2)}) async-start(), calls=%async_computation | async-start | bytes 1114112 | tf_op jit(solution)/shard_map/all_gather | solution.py:58
  10.2 142.2 %all-gather.5.cloned.1.call-start = ((), (), s32[]{:S(2)}) async-start(), calls=%async_computation.1 | async-start | bytes 2228224 | tf_op jit(solution)/shard_map/all_gather | solution.py:58
  68.6 3.2 %copy-start = (bf16[2048,256]{1,0:T(8,128)(2,1)S(1)}, bf16[2048,256]{1,0:T(8,128)(2,1)}, u32[]{:S(2)}) copy-start(bf16[2048,256]{1,0:T(8,128)(2,1)} %all-gather.3.cloned.1.call-done) | copy-start | bytes 3145732
  71.8 3.0 %copy-start.3 = (f32[128,256]{1,0:T(8,128)S(1)}, f32[128,256]{1,0:T(8,128)}, u32[]{:S(2)}) copy-start(f32[128,256]{1,0:T(8,128)} %param.12) | copy-start | bytes 393220
  84.7 4.0 %copy-start.4 = (s32[64,2,6]{0,1,2:T(2,128)S(1)}, s32[64,2,6]{0,1,2:T(2,128)}, u32[]{:S(2)}) copy-start(s32[64,2,6]{0,1,2:T(2,128)} %param.17) | copy-start | bytes 9220
  84.7 4.3 %copy-start.5 = (s32[64,2,6]{0,1,2:T(2,128)S(1)}, s32[64,2,6]{0,1,2:T(2,128)}, u32[]{:S(2)}) copy-start(s32[64,2,6]{0,1,2:T(2,128)} %param.19) | copy-start | bytes 9220
  85.1 4.6 %copy-start.6 = (f32[64,2,6]{0,1,2:T(2,128)S(1)}, f32[64,2,6]{0,1,2:T(2,128)}, u32[]{:S(2)}) copy-start(f32[64,2,6]{0,1,2:T(2,128)} %param.18) | copy-start | bytes 9220
  157.8 2.8 %copy-start.2 = (f32[64,256]{1,0:T(8,128)S(1)}, f32[64,256]{1,0:T(8,128)}, u32[]{:S(2)}) copy-start(f32[64,256]{1,0:T(8,128)} %param.13) | copy-start | bytes 196612
  160.4 3.2 %copy-start.1 = (bf16[4096,256]{0,1:T(8,128)(2,1)S(1)}, bf16[4096,256]{0,1:T(8,128)(2,1)}, u32[]{:S(2)}) copy-start(bf16[4096,256]{0,1:T(8,128)(2,1)} %all-gather.5.cloned.1.call-done) | copy-start | bytes 6291460
Sparse Core Ops, SparseCore 0:
  10.7 57.7 all-gather.2
  88.8 63.5 all-gather.4
where the time goes:
time: 183 us
  waiting for transfers between devices  116 us (63%)
  local copies, waits for them, and re-layouts  22.3 us (12%)
  matrix products  17.6 us (10%)
  between operations  14.7 us (8%)
  other arithmetic  8.43 us (5%)
  blocking collectives  4.18 us (2%)
    all_gather x2, waiting for transfers between devices, half_step(): whole = lax.all_gather(stacked, 'dev', axis=0, tiled=True)  116 us
    gather x8, local copies, waits for them, and re-layouts, collect(): picked = jnp.take(whole, row_index, axis=0).astype(jnp.float32)  10 us
    dot_general x6, matrix products, apply(): jnp.einsum('usr,ur->us', rows, vector, precision=lax.Precision.HIGHEST)  6.93 us
    dot_general x10, matrix products, apply(): jnp.dot(vector, gram, precision=lax.Precision.HIGHEST) + ridge * vector  4.72 us
    unnamed x9, other arithmetic  4.36 us
    all_gather x2, blocking collectives, half_step(): stacked = lax.all_gather(packed, 'grp', axis=0, tiled=True)  4.18 us
    dot_general x5, matrix products, apply(): jnp.einsum('us,usr->ur', weight * along, rows, precision=lax.Precision.HI...  3.94 us
  transfers between devices with their start and end apart: 2, of which 2 were waited for; matrix products, arithmetic and copies ran while one was open for 3% of the time, Pallas kernels for 0%

commit v1 on v0

v1 whole, which is shorter than its diff:
```python
import functools

import jax
import jax.numpy as jnp
from jax import lax
from jax.experimental import pallas as pl
from jax.experimental.pallas import tpu as pltpu
from jax.sharding import PartitionSpec as P

CG_STEPS = 4
RIDGE = 1.0
VMEM_LIMIT = 60 * 1024 * 1024


def swap(value, axis, bit):
    size = lax.axis_size(axis)
    return lax.ppermute(value, axis, [(i, i ^ bit) for i in range(size)])


def bits_of(size):
    return [1 << b for b in range(size.bit_length() - 1)]


def gather_pieces(own):
    rows = own.shape[0]
    low = [b for b in bits_of(lax.axis_size("dev")) if b <= 2]
    high = [b for b in bits_of(lax.axis_size("dev")) if b > 2]
    block, offsets = own, [0]
    for bit in high:
        block = jnp.concatenate([block, swap(block, "dev", bit)], axis=0)
        offsets = offsets + [o ^ bit for o in offsets]
    half = rows // 2
    shaped = block.reshape(len(offsets), rows, -1)
    parts = [
        shaped[:, :half].reshape(len(offsets) * half, -1),
        shaped[:, half:].reshape(len(offsets) * half, -1),
    ]
    marks = [list(offsets), list(offsets)]
    orders = [low, low[::-1]]
    for step in range(len(low)):
        for which in range(2):
            bit = orders[which][step]
            parts[which] = jnp.concatenate(
                [parts[which], swap(parts[which], "dev", bit)], axis=0
            )
            marks[which] = marks[which] + [o ^ bit for o in marks[which]]
    joined = jnp.concatenate(parts, axis=0)
    layout = [(0, o, 0, half) for o in marks[0]] + [(0, o, half, half) for o in marks[1]]
    pieces = [(joined, layout)]
    for bit in bits_of(lax.axis_size("grp")):
        pieces = pieces + [
            (swap(array, "grp", bit), [(g ^ bit, d, r, c) for g, d, r, c in layout])
            for array, layout in pieces
        ]
    return pieces


def split(value):
    high = value.astype(jnp.bfloat16)
    low = (value - high.astype(jnp.float32)).astype(jnp.bfloat16)
    return high, low


def dot(left, right):
    return jnp.dot(left, right, preferred_element_type=jnp.float32)


def solve_kernel(layouts, rows, devs, slots, *refs):
    count = len(layouts)
    ids_ref, start_ref, conf_ref, mask_ref = refs[:4]
    piece_refs = refs[4 : 4 + count]
    out_ref, packed_ref, table_ref, rows_ref = refs[4 + count :]
    users, rank = start_ref.shape
    me_grp, me_dev = lax.axis_index("grp"), lax.axis_index("dev")
    gram = jnp.zeros((rank, rank), jnp.float32)
    for ref, layout in zip(piece_refs, layouts):
        at = 0
        for g, d, first, length in layout:
            owner = (me_grp ^ g) * devs + (me_dev ^ d)
            where = pl.multiple_of(owner * rows + first, 8)
            table_ref[pl.ds(where, length), :] = ref[at : at + length, :].astype(jnp.float32)
            at += length
        block = ref[...]
        gram = gram + lax.dot_general(
            block, block, (((0,), (0,)), ((), ())), preferred_element_type=jnp.float32
        )

    total = rows_ref.shape[0]
    stride = total // slots * 0 + devs * rows
    per_block = slots

    def fetch(user, carry):
        for s in range(total):
            span = s // per_block
            where = ids_ref[user * total + s] + span * stride
            rows_ref[s, pl.ds(user, 1), :] = table_ref[pl.ds(where, 1), :]
        return carry

    lax.fori_loop(0, users, fetch, 0, unroll=8)

    gram_high, gram_low = split(gram)
    mask = mask_ref[...].astype(jnp.float32)
    weight = conf_ref[...] * mask
    gain = mask + weight

    def image_of(vector):
        high, low = split(vector)
        base = dot(high, gram_high) + dot(low, gram_high) + dot(high, gram_low)
        return base + RIDGE * vector

    def along(vector, s):
        return jnp.sum(rows_ref[s] * vector, axis=1, keepdims=True)

    x = start_ref[...]
    resid = -image_of(x)
    for s in range(total):
        scale = gain[:, s : s + 1] - weight[:, s : s + 1] * along(x, s)
        resid = resid + scale * rows_ref[s]
    direction = resid
    norm_now = jnp.sum(resid * resid, axis=1, keepdims=True)
    for step in range(CG_STEPS):
        image = image_of(direction)
        for s in range(total):
            image = image + (weight[:, s : s + 1] * along(direction, s)) * rows_ref[s]
        alpha = norm_now / jnp.sum(direction * image, axis=1, keepdims=True)
        x = x + alpha * direction
        if step + 1 < CG_STEPS:
            resid = resid - alpha * image
            norm_next = jnp.sum(resid * resid, axis=1, keepdims=True)
            direction = resid + (norm_next / norm_now) * direction
            norm_now = norm_next
    out_ref[...] = x
    packed_ref[...] = x.astype(jnp.bfloat16)


def half_step(start_x, packed, slot_ids, confidence, slot_mask):
    users, rank = start_x.shape
    rows = packed.shape[0]
    groups, devs = lax.axis_size("grp"), lax.axis_size("dev")
    slots = slot_ids.shape[2]
    total = groups * slots
    pieces = gather_pieces(packed)
    vmem = pl.BlockSpec(memory_space=pltpu.VMEM)
    return pl.pallas_call(
        functools.partial(solve_kernel, [p[1] for p in pieces], rows, devs, slots),
        out_shape=(
            jax.ShapeDtypeStruct((users, rank), jnp.float32),
            jax.ShapeDtypeStruct((users, rank), jnp.bfloat16),
        ),
        in_specs=[pl.BlockSpec(memory_space=pltpu.SMEM)] + [vmem] * (3 + len(pieces)),
        out_specs=(vmem, vmem),
        scratch_shapes=[
            pltpu.VMEM((groups * devs * rows, rank), jnp.float32),
            pltpu.VMEM((total, users, rank), jnp.float32),
        ],
        compiler_params=pltpu.CompilerParams(vmem_limit_bytes=VMEM_LIMIT),
    )(
        slot_ids.reshape(-1),
        start_x,
        confidence.reshape(users, total),
        slot_mask.reshape(users, total),
        *[p[0] for p in pieces],
    )


def per_device(
    user_factors, item_factors, user_items, user_conf, user_mask, item_users, item_conf, item_mask
):
    new_users, packed = half_step(
        user_factors, item_factors.astype(jnp.bfloat16), user_items, user_conf, user_mask
    )
    new_items, _ = half_step(item_factors, packed, item_users, item_conf, item_mask)
    return (new_users, new_items)


def solution(mesh):
    rows2 = P(("grp", "dev"), None)
    rows3 = P(("grp", "dev"), None, None)
    return jax.shard_map(
        per_device,
        mesh=mesh,
        in_specs=(rows2, rows2) + (rows3,) * 6,
        out_specs=(rows2, rows2),
        check_vma=False,
    )
```

time: 183 us -> 81.7 us (0.45)
  waiting for transfers between devices: 116 us -> 27.8 us
  starting transfers between devices: 0.08 us -> 22.2 us
  Pallas kernels: 0 us -> 22 us
  matrix products: 17.6 us -> 0 us
  local copies, waits for them, and re-layouts: 22.3 us -> 6.77 us
  between operations: 14.7 us -> 0.86 us
  other arithmetic: 8.43 us -> 1.78 us
  blocking collectives: 4.18 us -> 0 us
    all_gather x2 -> x0, waiting for transfers between devices: 116 us -> none  [half_step(): whole = lax.all_gather(stacked, 'dev', axis=0, tiled=True)]
    ppermute x0 -> x14, waiting for transfers between devices: none -> 27.8 us  [swap(): return lax.ppermute(value, axis, [(i, i ^ bit) for i in range(size)])]
    ppermute x0 -> x14, starting transfers between devices: none -> 22.2 us  [swap(): return lax.ppermute(value, axis, [(i, i ^ bit) for i in range(size)])]
    pallas_call x0 -> x2, Pallas kernels: none -> 22 us  [half_step(): pl.pallas_call(functools.partial(solve_kernel, [p[1] for p in pieces], ro...]
    dot_general x24 -> x0, matrix products: 17.6 us -> none  [the longest x6 6.93 us: apply(): jnp.einsum('usr,ur->us', rows, vector, precision=lax.Precision.HIGHEST)]
    gather x8 -> x0, local copies, waits for them, and re-layouts: 10 us -> none  [collect(): picked = jnp.take(whole, row_index, axis=0).astype(jnp.float32)]
    reshape x0 -> x10, local copies, waits for them, and re-layouts: none -> 4.52 us  [the longest x2 1.6 us: half_step(): slot_ids.reshape(-1)]
    unnamed x9 -> x0, other arithmetic: 4.36 us -> none
  transfers between devices with their start and end apart: 2 -> 14, of which waited for: 2 -> 12; matrix products, arithmetic and copies ran while one was open for 3% -> 6% of each run, Pallas kernels for 0% -> 0%
where the time goes in v1:
time: 81.7 us; the launch traced here: 81.4 us
  waiting for transfers between devices  27.8 us (34%)
  starting transfers between devices  22.2 us (27%)
  Pallas kernels  22 us (27%)
  local copies, waits for them, and re-layouts  6.77 us (8%)
  other arithmetic  1.78 us (2%)
  between operations  0.86 us (1%)
    ppermute x14, waiting for transfers between devices, swap(): return lax.ppermute(value, axis, [(i, i ^ bit) for i in range(size)])  27.8 us
    ppermute x14, starting transfers between devices, swap(): return lax.ppermute(value, axis, [(i, i ^ bit) for i in range(size)])  22.2 us
    pallas_call x2, Pallas kernels, half_step(): pl.pallas_call(functools.partial(solve_kernel, [p[1] for p in pieces], ro...  22 us
    unnamed x38, local copies, waits for them, and re-layouts  2.19 us
  transfers between devices with their start and end apart: 14, of which 12 were waited for; matrix products, arithmetic and copies ran while one was open for 6% of the time, Pallas kernels for 0%

profile of v1, /device:TPU:0, one launch (start us, length us, event | category | flops | bytes accessed | tf_op | source)
XLA Modules:
  0.0 81.4 jit_solution(80989436621156628)
XLA Ops:
  0.6 0.8 %convert_element_type.3 = bf16[64,256]{1,0:T(8,128)(2,1)S(1)} convert(f32[64,256]{1,0:T(8,128)} %refs_1_.3) | non-fusion elementwise | flops 16384 | bytes 98304 | tf_op jit(solution)/shard_map/convert_element_type | solution.py:170
  1.5 3.1 %collective-permute-start = (bf16[64,256]{1,0:T(8,128)(2,1)S(1)}, bf16[64,256]{1,0:T(8,128)(2,1)S(1)}, u32[]{:S(2)}, u32[]{:S(2)}) collective-permute-start(bf16[64,256]{1,0:T(8,128)(2,1)S(1)} %convert_element_type.3), channel_id=1, source_target_pairs={{0,4},{1,5},{2,6},{3,7},{4,0},{5,1},{6,2},{7,3},{8,12},{9,13},{10,... | collective-permute-start | bytes 98312 | tf_op jit(solution)/shard_map/ppermute | solution.py:17
  4.5 1.9 %collective-permute-done = bf16[64,256]{1,0:T(8,128)(2,1)S(1)} collective-permute-done((bf16[64,256]{1,0:T(8,128)(2,1)S(1)}, bf16[64,256]{1,0:T(8,128)(2,1)S(1)}, u32[]{:S(2)}, u32[]{:S(2)}) %collective-permute-start) | collective-permute-done | bytes 32800 | tf_op jit(solution)/shard_map/ppermute | solution.py:17
  6.4 3.0 %collective-permute-start.1 = (bf16[128,256]{1,0:T(8,128)(2,1)S(1)}, bf16[128,256]{1,0:T(8,128)(2,1)S(1)}, u32[]{:S(2)}, u32[]{:S(2)}) collective-permute-start(bf16[128,256]{1,0:T(8,128)(2,1)S(1)} %pad_maximum_fusion.7), channel_id=1, source_target_pairs={{0,8},{1,9},{2,10},{3,11},{4,12},{5,13},{6,14},{7,15},{8,0},{9,1},... | collective-permute-start | bytes 196616 | tf_op jit(solution)/shard_map/ppermute | solution.py:17
  9.5 2.2 %collective-permute-done.1 = bf16[128,256]{1,0:T(8,128)(2,1)S(1)} collective-permute-done((bf16[128,256]{1,0:T(8,128)(2,1)S(1)}, bf16[128,256]{1,0:T(8,128)(2,1)S(1)}, u32[]{:S(2)}, u32[]{:S(2)}) %collective-permute-start.1) | collective-permute-done | bytes 65568 | tf_op jit(solution)/shard_map/ppermute | solution.py:17
  11.7 1.9 %collective-permute-start.2 = (bf16[128,256]{1,0:T(8,128)(2,1)S(1)}, bf16[128,256]{1,0:T(8,128)(2,1)S(1)}, u32[]{:S(2)}, u32[]{:S(2)}) collective-permute-start(bf16[128,256]{1,0:T(8,128)(2,1)S(1)} %bitcast.24), channel_id=1, source_target_pairs={{0,1},{1,0},{2,3},{3,2},{4,5},{5,4},{6,7},{7,6},{8,9},{9,8},{10,11... | collective-permute-start | bytes 196616 | tf_op jit(solution)/shard_map/ppermute | solution.py:17
  13.6 1.5 %collective-permute-start.4 = (bf16[128,256]{1,0:T(8,128)(2,1)S(1)}, bf16[128,256]{1,0:T(8,128)(2,1)S(1)}, u32[]{:S(2)}, u32[]{:S(2)}) collective-permute-start(bf16[128,256]{1,0:T(8,128)(2,1)S(1)} %bitcast.21), channel_id=1, source_target_pairs={{0,2},{1,3},{2,0},{3,1},{4,6},{5,7},{6,4},{7,5},{8,10},{9,11},{10,... | collective-permute-start | bytes 196616 | tf_op jit(solution)/shard_map/ppermute | solution.py:17
  15.2 0.9 %collective-permute-done.2 = bf16[128,256]{1,0:T(8,128)(2,1)S(1)} collective-permute-done((bf16[128,256]{1,0:T(8,128)(2,1)S(1)}, bf16[128,256]{1,0:T(8,128)(2,1)S(1)}, u32[]{:S(2)}, u32[]{:S(2)}) %collective-permute-start.2) | collective-permute-done | bytes 65568 | tf_op jit(solution)/shard_map/ppermute | solution.py:17
  16.1 1.9 %collective-permute-start.3 = (bf16[256,256]{1,0:T(8,128)(2,1)S(1)}, bf16[256,256]{1,0:T(8,128)(2,1)S(1)}, u32[]{:S(2)}, u32[]{:S(2)}) collective-permute-start(bf16[256,256]{1,0:T(8,128)(2,1)S(1)} %pad_maximum_fusion.4), channel_id=1, source_target_pairs={{0,2},{1,3},{2,0},{3,1},{4,6},{5,7},{6,4},{7,5},{8,10},{9,11},{10,... | collective-permute-start | bytes 393224 | tf_op jit(solution)/shard_map/ppermute | solution.py:17
  18.0 0.0 collective-permute-done.4
  18.0 2.2 %collective-permute-start.5 = (bf16[256,256]{1,0:T(8,128)(2,1)S(1)}, bf16[256,256]{1,0:T(8,128)(2,1)S(1)}, u32[]{:S(2)}, u32[]{:S(2)}) collective-permute-start(bf16[256,256]{1,0:T(8,128)(2,1)S(1)} %pad_maximum_fusion.5), channel_id=1, source_target_pairs={{0,1},{1,0},{2,3},{3,2},{4,5},{5,4},{6,7},{7,6},{8,9},{9,8},{10,11... | collective-permute-start | bytes 393224 | tf_op jit(solution)/shard_map/ppermute | solution.py:17
  20.2 0.9 %collective-permute-done.3 = bf16[256,256]{1,0:T(8,128)(2,1)S(1)} collective-permute-done((bf16[256,256]{1,0:T(8,128)(2,1)S(1)}, bf16[256,256]{1,0:T(8,128)(2,1)S(1)}, u32[]{:S(2)}, u32[]{:S(2)}) %collective-permute-start.3) | collective-permute-done | bytes 131104 | tf_op jit(solution)/shard_map/ppermute | solution.py:17
  21.2 0.0 copy-start.10
  21.2 2.0 %collective-permute-done.5 = bf16[256,256]{1,0:T(8,128)(2,1)S(1)} collective-permute-done((bf16[256,256]{1,0:T(8,128)(2,1)S(1)}, bf16[256,256]{1,0:T(8,128)(2,1)S(1)}, u32[]{:S(2)}, u32[]{:S(2)}) %collective-permute-start.5) | collective-permute-done | bytes 131104 | tf_op jit(solution)/shard_map/ppermute | solution.py:17
  23.2 0.0 copy-start.2
  23.2 0.1 collective-permute-start.6
  23.3 0.0 copy-done.10
  23.3 0.2 copy.14
  23.4 0.0 copy-start.8
  23.4 0.8 reshape.40.refs_0_
  24.2 0.0 copy-done.8
  24.3 0.0 copy-start.9
  24.3 0.7 copy.17.refs_2_
  25.0 0.0 copy-done.9
  25.0 0.7 copy.18.refs_3_
  25.8 0.0 collective-permute-done.6.refs_5_
  25.8 0.0 copy-done.2
  25.8 0.0 copy-start.3
  25.8 0.8 %copy-done.3 = bf16[1024,256]{1,0:T(8,128)(2,1)} copy-done((bf16[1024,256]{1,0:T(8,128)(2,1)}, bf16[1024,256]{1,0:T(8,128)(2,1)S(1)}, u32[]{:S(2)}) %copy-start.3) | copy-done | bytes 524312
  26.6 9.3 %shard_map.95 = (f32[128,256]{1,0:T(8,128)}, bf16[128,256]{1,0:T(8,128)(2,1)}) custom-call(s32[768]{0:T(1024)} %reshape.40.refs_0_, f32[128,256]{1,0:T(8,128)} %refs_1_.2, f32[128,6]{1,0:T(8,128)} %copy.17.refs_2_, s32[128,6]{1,0:T(8,128)} %copy.18.refs_3_, bf16[1024,256]{1,0:T(8,128)(2,1)} %copy-done.2, bf16[1024,256]{1,0:T(8,128)(2,1)} %copy-done.3), custom_call_target="tpu_custom_call" | custom-call | tf_op jit(solution)/shard_map/pallas_call | solution.py:144
  35.9 0.0 copy-start.4
  35.9 1.5 %collective-permute-start.7 = (bf16[128,256]{1,0:T(8,128)(2,1)}, bf16[128,256]{1,0:T(8,128)(2,1)S(1)}, u32[]{:S(2)}, u32[]{:S(2)}) collective-permute-start(bf16[128,256]{1,0:T(8,128)(2,1)} %get-tuple-element.6), channel_id=1, source_target_pairs={{0,4},{1,5},{2,6},{3,7},{4,0},{5,1},{6,2},{7,3},{8,12},{9,13},{10,... | collective-permute-start | bytes 196616 | tf_op jit(solution)/shard_map/ppermute | solution.py:17
  37.4 3.2 %collective-permute-done.7 = bf16[128,256]{1,0:T(8,128)(2,1)S(1)} collective-permute-done((bf16[128,256]{1,0:T(8,128)(2,1)}, bf16[128,256]{1,0:T(8,128)(2,1)S(1)}, u32[]{:S(2)}, u32[]{:S(2)}) %collective-permute-start.7) | collective-permute-done | bytes 65568 | tf_op jit(solution)/shard_map/ppermute | solution.py:17
  40.6 0.8 %pad_maximum_fusion.6 = bf16[256,256]{1,0:T(8,128)(2,1)S(1)} fusion(bf16[128,256]{1,0:T(8,128)(2,1)S(1)} %collective-permute-done.7, bf16[128,256]{1,0:T(8,128)(2,1)} %get-tuple-element.6), kind=kLoop, calls=%fused_computation.6 | loop fusion | flops 262144 | bytes 262144 | tf_op jit(solution)/shard_map/concatenate | solution.py:30
  41.5 3.1 %collective-permute-start.8 = (bf16[256,256]{1,0:T(8,128)(2,1)S(1)}, bf16[256,256]{1,0:T(8,128)(2,1)S(1)}, u32[]{:S(2)}, u32[]{:S(2)}) collective-permute-start(bf16[256,256]{1,0:T(8,128)(2,1)S(1)} %pad_maximum_fusion.6), channel_id=1, source_target_pairs={{0,8},{1,9},{2,10},{3,11},{4,12},{5,13},{6,14},{7,15},{8,0},{9,1},... | collective-permute-start | bytes 393224 | tf_op jit(solution)/shard_map/ppermute | solution.py:17
  44.6 6.4 %collective-permute-done.8 = bf16[256,256]{1,0:T(8,128)(2,1)S(1)} collective-permute-done((bf16[256,256]{1,0:T(8,128)(2,1)S(1)}, bf16[256,256]{1,0:T(8,128)(2,1)S(1)}, u32[]{:S(2)}, u32[]{:S(2)}) %collective-permute-start.8) | collective-permute-done | bytes 131104 | tf_op jit(solution)/shard_map/ppermute | solution.py:17
  51.0 0.0 copy-done.4
  51.0 2.1 %collective-permute-start.9 = (bf16[256,256]{1,0:T(8,128)(2,1)S(1)}, bf16[256,256]{1,0:T(8,128)(2,1)S(1)}, u32[]{:S(2)}, u32[]{:S(2)}) collective-permute-start(bf16[256,256]{1,0:T(8,128)(2,1)S(1)} %bitcast.17), channel_id=1, source_target_pairs={{0,1},{1,0},{2,3},{3,2},{4,5},{5,4},{6,7},{7,6},{8,9},{9,8},{10,11... | collective-permute-start | bytes 393224 | tf_op jit(solution)/shard_map/ppermute | solution.py:17
  53.1 0.4 collective-permute-start.11
  53.5 2.6 %collective-permute-done.9 = bf16[256,256]{1,0:T(8,128)(2,1)S(1)} collective-permute-done((bf16[256,256]{1,0:T(8,128)(2,1)S(1)}, bf16[256,256]{1,0:T(8,128)(2,1)S(1)}, u32[]{:S(2)}, u32[]{:S(2)}) %collective-permute-start.9) | collective-permute-done | bytes 131104 | tf_op jit(solution)/shard_map/ppermute | solution.py:17
  56.1 1.3 %collective-permute-start.10 = (bf16[512,256]{1,0:T(8,128)(2,1)S(1)}, bf16[512,256]{1,0:T(8,128)(2,1)S(1)}, u32[]{:S(2)}, u32[]{:S(2)}) collective-permute-start(bf16[512,256]{1,0:T(8,128)(2,1)S(1)} %pad_maximum_fusion.1), channel_id=1, source_target_pairs={{0,2},{1,3},{2,0},{3,1},{4,6},{5,7},{6,4},{7,5},{8,10},{9,11},{10,... | collective-permute-start | bytes 786440 | tf_op jit(solution)/shard_map/ppermute | solution.py:17
  57.5 1.1 %collective-permute-done.11 = bf16[256,256]{1,0:T(8,128)(2,1)S(1)} collective-permute-done((bf16[256,256]{1,0:T(8,128)(2,1)S(1)}, bf16[256,256]{1,0:T(8,128)(2,1)S(1)}, u32[]{:S(2)}, u32[]{:S(2)}) %collective-permute-start.11) | collective-permute-done | bytes 131104 | tf_op jit(solution)/shard_map/ppermute | solution.py:17
  58.6 0.1 collective-permute-start.12
  58.7 5.0 %collective-permute-done.10 = bf16[512,256]{1,0:T(8,128)(2,1)S(1)} collective-permute-done((bf16[512,256]{1,0:T(8,128)(2,1)S(1)}, bf16[512,256]{1,0:T(8,128)(2,1)S(1)}, u32[]{:S(2)}, u32[]{:S(2)}) %collective-permute-start.10) | collective-permute-done | bytes 262176 | tf_op jit(solution)/shard_map/ppermute | solution.py:17
  63.8 0.0 copy-start.5
  63.8 1.3 %collective-permute-done.12 = bf16[512,256]{1,0:T(8,128)(2,1)S(1)} collective-permute-done((bf16[512,256]{1,0:T(8,128)(2,1)S(1)}, bf16[512,256]{1,0:T(8,128)(2,1)S(1)}, u32[]{:S(2)}, u32[]{:S(2)}) %collective-permute-start.12) | collective-permute-done | bytes 262176 | tf_op jit(solution)/shard_map/ppermute | solution.py:17
  65.1 0.0 copy-start
  65.1 0.1 collective-permute-start.13
  65.2 0.0 copy-done.5
  65.2 0.1 copy.19
  65.3 0.0 copy-start.6
  65.3 0.8 reshape.46.refs_0_
  66.1 0.0 copy-done.6
  66.1 0.0 copy-start.7
  66.1 0.7 copy.22.refs_2_
  66.9 0.0 copy-done.7
  66.9 0.7 copy.23.refs_3_
  67.6 0.3 collective-permute-done.13.refs_5_
  67.8 0.0 copy-done
  67.8 0.0 copy-start.1
  67.8 1.0 %copy-done.1 = bf16[2048,256]{1,0:T(8,128)(2,1)} copy-done((bf16[2048,256]{1,0:T(8,128)(2,1)}, bf16[2048,256]{1,0:T(8,128)(2,1)S(1)}, u32[]{:S(2)}) %copy-start.1) | copy-done | bytes 1048600
  68.8 12.6 %shard_map.96 = (f32[64,256]{1,0:T(8,128)}, bf16[64,256]{1,0:T(8,128)(2,1)}) custom-call(s32[768]{0:T(1024)} %reshape.46.refs_0_, f32[64,256]{1,0:T(8,128)} %refs_1_.3, f32[64,12]{1,0:T(8,128)} %copy.22.refs_2_, s32[64,12]{1,0:T(8,128)} %copy.23.refs_3_, bf16[2048,256]{1,0:T(8,128)(2,1)} %copy-done, bf16[2048,256]{1,0:T(8,128)(2,1)} %copy-done.1), custom_call_target="tpu_custom_call" | custom-call | tf_op jit(solution)/shard_map/pallas_call | solution.py:144
  (29 shorter events, 0.3 us)
Async XLA Ops:
  1.5 4.9 %collective-permute-start = (bf16[64,256]{1,0:T(8,128)(2,1)S(1)}, bf16[64,256]{1,0:T(8,128)(2,1)S(1)}, u32[]{:S(2)}, u32[]{:S(2)}) collective-permute-start(bf16[64,256]{1,0:T(8,128)(2,1)S(1)} %convert_element_type.3), channel_id=1, source_target_pairs={{0,4},{1,5},{2,6},{3,7},{4,0},{5,1},{6,2},{7,3},{8,12},{9,13},{10,... | collective-permute-start | bytes 98312 | tf_op jit(solution)/shard_map/ppermute | solution.py:17
  6.4 5.3 %collective-permute-start.1 = (bf16[128,256]{1,0:T(8,128)(2,1)S(1)}, bf16[128,256]{1,0:T(8,128)(2,1)S(1)}, u32[]{:S(2)}, u32[]{:S(2)}) collective-permute-start(bf16[128,256]{1,0:T(8,128)(2,1)S(1)} %pad_maximum_fusion.7), channel_id=1, source_target_pairs={{0,8},{1,9},{2,10},{3,11},{4,12},{5,13},{6,14},{7,15},{8,0},{9,1},... | collective-permute-start | bytes 196616 | tf_op jit(solution)/shard_map/ppermute | solution.py:17
  11.7 4.3 %collective-permute-start.2 = (bf16[128,256]{1,0:T(8,128)(2,1)S(1)}, bf16[128,256]{1,0:T(8,128)(2,1)S(1)}, u32[]{:S(2)}, u32[]{:S(2)}) collective-permute-start(bf16[128,256]{1,0:T(8,128)(2,1)S(1)} %bitcast.24), channel_id=1, source_target_pairs={{0,1},{1,0},{2,3},{3,2},{4,5},{5,4},{6,7},{7,6},{8,9},{9,8},{10,11... | collective-permute-start | bytes 196616 | tf_op jit(solution)/shard_map/ppermute | solution.py:17
  13.6 4.4 %collective-permute-start.4 = (bf16[128,256]{1,0:T(8,128)(2,1)S(1)}, bf16[128,256]{1,0:T(8,128)(2,1)S(1)}, u32[]{:S(2)}, u32[]{:S(2)}) collective-permute-start(bf16[128,256]{1,0:T(8,128)(2,1)S(1)} %bitcast.21), channel_id=1, source_target_pairs={{0,2},{1,3},{2,0},{3,1},{4,6},{5,7},{6,4},{7,5},{8,10},{9,11},{10,... | collective-permute-start | bytes 196616 | tf_op jit(solution)/shard_map/ppermute | solution.py:17
  16.1 5.0 %collective-permute-start.3 = (bf16[256,256]{1,0:T(8,128)(2,1)S(1)}, bf16[256,256]{1,0:T(8,128)(2,1)S(1)}, u32[]{:S(2)}, u32[]{:S(2)}) collective-permute-start(bf16[256,256]{1,0:T(8,128)(2,1)S(1)} %pad_maximum_fusion.4), channel_id=1, source_target_pairs={{0,2},{1,3},{2,0},{3,1},{4,6},{5,7},{6,4},{7,5},{8,10},{9,11},{10,... | collective-permute-start | bytes 393224 | tf_op jit(solution)/shard_map/ppermute | solution.py:17
  18.0 5.1 %collective-permute-start.5 = (bf16[256,256]{1,0:T(8,128)(2,1)S(1)}, bf16[256,256]{1,0:T(8,128)(2,1)S(1)}, u32[]{:S(2)}, u32[]{:S(2)}) collective-permute-start(bf16[256,256]{1,0:T(8,128)(2,1)S(1)} %pad_maximum_fusion.5), channel_id=1, source_target_pairs={{0,1},{1,0},{2,3},{3,2},{4,5},{5,4},{6,7},{7,6},{8,9},{9,8},{10,11... | collective-permute-start | bytes 393224 | tf_op jit(solution)/shard_map/ppermute | solution.py:17
  21.2 2.1 %copy-start.10 = (s32[128,2,3]{0,1,2:T(2,128)S(1)}, s32[128,2,3]{0,1,2:T(2,128)}, u32[]{:S(2)}) copy-start(s32[128,2,3]{0,1,2:T(2,128)} %param.10) | copy-start | bytes 9220
  23.2 2.6 %copy-start.2 = (bf16[1024,256]{1,0:T(8,128)(2,1)}, bf16[1024,256]{1,0:T(8,128)(2,1)S(1)}, u32[]{:S(2)}) copy-start(bf16[1024,256]{1,0:T(8,128)(2,1)S(1)} %constant_dynamic-update-slice_fusion.refs_4_) | copy-start | bytes 1572868
  23.2 2.6 %collective-permute-start.6 = (bf16[1024,256]{1,0:T(8,128)(2,1)S(1)}, bf16[1024,256]{1,0:T(8,128)(2,1)S(1)}, u32[]{:S(2)}, u32[]{:S(2)}) collective-permute-start(bf16[1024,256]{1,0:T(8,128)(2,1)S(1)} %constant_dynamic-update-slice_fusion.refs_4_), channel_id=1, source_target_pairs={{0,16},{16,0},{1,17},{17,1},{2,18},{18,2},{3,19},{19,3},{4,20},{20... | collective-permute-start | bytes 1572872 | tf_op jit(solution)/shard_map/ppermute | solution.py:17
  23.4 0.8 %copy-start.8 = (f32[128,2,3]{0,1,2:T(2,128)S(1)}, f32[128,2,3]{0,1,2:T(2,128)}, u32[]{:S(2)}) copy-start(f32[128,2,3]{0,1,2:T(2,128)} %param.11) | copy-start | bytes 9220
  24.3 0.7 copy-start.9
  25.8 0.8 %copy-start.3 = (bf16[1024,256]{1,0:T(8,128)(2,1)}, bf16[1024,256]{1,0:T(8,128)(2,1)S(1)}, u32[]{:S(2)}) copy-start(bf16[1024,256]{1,0:T(8,128)(2,1)S(1)} %collective-permute-done.6.refs_5_) | copy-start | bytes 1572868
  35.9 15.1 %copy-start.4 = (bf16[128,256]{1,0:T(8,128)(2,1)S(1)}, bf16[128,256]{1,0:T(8,128)(2,1)}, u32[]{:S(2)}) copy-start(bf16[128,256]{1,0:T(8,128)(2,1)} %get-tuple-element.6) | copy-start | bytes 196612
  35.9 4.7 %collective-permute-start.7 = (bf16[128,256]{1,0:T(8,128)(2,1)}, bf16[128,256]{1,0:T(8,128)(2,1)S(1)}, u32[]{:S(2)}, u32[]{:S(2)}) collective-permute-start(bf16[128,256]{1,0:T(8,128)(2,1)} %get-tuple-element.6), channel_id=1, source_target_pairs={{0,4},{1,5},{2,6},{3,7},{4,0},{5,1},{6,2},{7,3},{8,12},{9,13},{10,... | collective-permute-start | bytes 196616 | tf_op jit(solution)/shard_map/ppermute | solution.py:17
  41.5 9.5 %collective-permute-start.8 = (bf16[256,256]{1,0:T(8,128)(2,1)S(1)}, bf16[256,256]{1,0:T(8,128)(2,1)S(1)}, u32[]{:S(2)}, u32[]{:S(2)}) collective-permute-start(bf16[256,256]{1,0:T(8,128)(2,1)S(1)} %pad_maximum_fusion.6), channel_id=1, source_target_pairs={{0,8},{1,9},{2,10},{3,11},{4,12},{5,13},{6,14},{7,15},{8,0},{9,1},... | collective-permute-start | bytes 393224 | tf_op jit(solution)/shard_map/ppermute | solution.py:17
  51.0 5.1 %collective-permute-start.9 = (bf16[256,256]{1,0:T(8,128)(2,1)S(1)}, bf16[256,256]{1,0:T(8,128)(2,1)S(1)}, u32[]{:S(2)}, u32[]{:S(2)}) collective-permute-start(bf16[256,256]{1,0:T(8,128)(2,1)S(1)} %bitcast.17), channel_id=1, source_target_pairs={{0,1},{1,0},{2,3},{3,2},{4,5},{5,4},{6,7},{7,6},{8,9},{9,8},{10,11... | collective-permute-start | bytes 393224 | tf_op jit(solution)/shard_map/ppermute | solution.py:17
  53.1 5.5 %collective-permute-start.11 = (bf16[256,256]{1,0:T(8,128)(2,1)S(1)}, bf16[256,256]{1,0:T(8,128)(2,1)S(1)}, u32[]{:S(2)}, u32[]{:S(2)}) collective-permute-start(bf16[256,256]{1,0:T(8,128)(2,1)S(1)} %bitcast.14), channel_id=1, source_target_pairs={{0,2},{1,3},{2,0},{3,1},{4,6},{5,7},{6,4},{7,5},{8,10},{9,11},{10,... | collective-permute-start | bytes 393224 | tf_op jit(solution)/shard_map/ppermute | solution.py:17
  56.1 7.6 %collective-permute-start.10 = (bf16[512,256]{1,0:T(8,128)(2,1)S(1)}, bf16[512,256]{1,0:T(8,128)(2,1)S(1)}, u32[]{:S(2)}, u32[]{:S(2)}) collective-permute-start(bf16[512,256]{1,0:T(8,128)(2,1)S(1)} %pad_maximum_fusion.1), channel_id=1, source_target_pairs={{0,2},{1,3},{2,0},{3,1},{4,6},{5,7},{6,4},{7,5},{8,10},{9,11},{10,... | collective-permute-start | bytes 786440 | tf_op jit(solution)/shard_map/ppermute | solution.py:17
  58.6 6.4 %collective-permute-start.12 = (bf16[512,256]{1,0:T(8,128)(2,1)S(1)}, bf16[512,256]{1,0:T(8,128)(2,1)S(1)}, u32[]{:S(2)}, u32[]{:S(2)}) collective-permute-start(bf16[512,256]{1,0:T(8,128)(2,1)S(1)} %pad_maximum_fusion.2), channel_id=1, source_target_pairs={{0,1},{1,0},{2,3},{3,2},{4,5},{5,4},{6,7},{7,6},{8,9},{9,8},{10,11... | collective-permute-start | bytes 786440 | tf_op jit(solution)/shard_map/ppermute | solution.py:17
  63.8 1.4 %copy-start.5 = (s32[64,2,6]{0,1,2:T(2,128)S(1)}, s32[64,2,6]{0,1,2:T(2,128)}, u32[]{:S(2)}) copy-start(s32[64,2,6]{0,1,2:T(2,128)} %param.13) | copy-start | bytes 9220
  65.1 2.7 %copy-start = (bf16[2048,256]{1,0:T(8,128)(2,1)}, bf16[2048,256]{1,0:T(8,128)(2,1)S(1)}, u32[]{:S(2)}) copy-start(bf16[2048,256]{1,0:T(8,128)(2,1)S(1)} %constant_dynamic-update-slice_fusion.6.refs_4_) | copy-start | bytes 3145732
  65.1 2.7 %collective-permute-start.13 = (bf16[2048,256]{1,0:T(8,128)(2,1)S(1)}, bf16[2048,256]{1,0:T(8,128)(2,1)S(1)}, u32[]{:S(2)}, u32[]{:S(2)}) collective-permute-start(bf16[2048,256]{1,0:T(8,128)(2,1)S(1)} %constant_dynamic-update-slice_fusion.6.refs_4_), channel_id=1, source_target_pairs={{0,16},{16,0},{1,17},{17,1},{2,18},{18,2},{3,19},{19,3},{4,20},{20... | collective-permute-start | bytes 3145736 | tf_op jit(solution)/shard_map/ppermute | solution.py:17
  65.3 0.8 %copy-start.6 = (f32[64,2,6]{0,1,2:T(2,128)S(1)}, f32[64,2,6]{0,1,2:T(2,128)}, u32[]{:S(2)}) copy-start(f32[64,2,6]{0,1,2:T(2,128)} %param.14) | copy-start | bytes 9220
  66.1 0.7 copy-start.7
  67.8 1.0 %copy-start.1 = (bf16[2048,256]{1,0:T(8,128)(2,1)}, bf16[2048,256]{1,0:T(8,128)(2,1)S(1)}, u32[]{:S(2)}) copy-start(bf16[2048,256]{1,0:T(8,128)(2,1)S(1)} %collective-permute-done.13.refs_5_) | copy-start | bytes 3145732

commit v2 on v1

v2 whole, which is shorter than its diff:
```python
import functools

import jax
import jax.numpy as jnp
from jax import lax
from jax.experimental import pallas as pl
from jax.experimental.pallas import tpu as pltpu
from jax.sharding import PartitionSpec as P

CG_STEPS = 4
RIDGE = 1.0
LANES = 128
MIB = 1024 * 1024


def swap(value, axis, bit):
    size = lax.axis_size(axis)
    return lax.ppermute(value, axis, [(i, i ^ bit) for i in range(size)])


def bits_of(size):
    return [1 << b for b in range(size.bit_length() - 1)]


def gather_pieces(own, axis):
    bits = bits_of(lax.axis_size("dev"))
    low = [b for b in bits if b <= 2]
    high = [b for b in bits if b > 2]
    block, marks = own, [0]
    for bit in high[::-1]:
        block = jnp.concatenate([block, swap(block, "dev", bit)], axis=axis)
        marks = marks + [o ^ bit for o in marks]
    pieces = [(block, marks)]
    if len(marks) > 1:
        half = len(marks) // 2
        pieces = list(zip(jnp.split(block, 2, axis=axis), (marks[:half], marks[half:])))
    orders = [low, low[::-1]]
    for step in range(len(low)):
        for which, (block, marks) in enumerate(pieces):
            bit = orders[which][step]
            block = jnp.concatenate([block, swap(block, "dev", bit)], axis=axis)
            pieces[which] = (block, marks + [o ^ bit for o in marks])
    pieces = [(block, [(0, o) for o in marks]) for block, marks in pieces]
    for bit in bits_of(lax.axis_size("grp")):
        pieces = pieces + [
            (swap(block, "grp", bit), [(g ^ bit, o) for g, o in marks]) for block, marks in pieces
        ]
    return pieces


def split(value):
    high = value.astype(jnp.bfloat16)
    low = (value - high.astype(jnp.float32)).astype(jnp.bfloat16)
    return high, low


def solve_kernel(marks, axis, rows, groups, *refs):
    count = len(marks)
    start_ref, ids_ref, conf_ref, mask_ref = refs[:4]
    piece_refs = refs[4 : 4 + count]
    out_ref, packed_ref, hot_ref, rows_ref, gram_ref = refs[4 + count :]
    users, rank = start_ref.shape
    slots = ids_ref.shape[0]
    pack = max(1, LANES // users)
    width = pack * users
    tiles = slots // pack
    me_grp, me_dev = lax.axis_index("grp"), lax.axis_index("dev")

    def row_of(ref, g, tile):
        block = me_grp ^ g
        parts = [ref[tile * pack + i, pl.ds(block, 1), :] for i in range(pack)]
        return parts[0] if pack == 1 else jnp.concatenate(parts, axis=1)

    weights, gains = [], []
    for g in range(groups):
        for tile in range(tiles):
            mask = row_of(mask_ref, g, tile).astype(jnp.float32)
            weight = row_of(conf_ref, g, tile) * mask
            weights.append(weight)
            gains.append(mask + weight)

    side = (((axis,), (axis,)), ((), ()))
    gram = jnp.zeros((rank, rank), jnp.float32)
    place = lax.broadcasted_iota(jnp.int32, (rows, width), 0)
    seen = set()
    for ref, mark in zip(piece_refs, marks):
        g = mark[0][0]
        for tile in range(tiles):
            ids = row_of(ids_ref, g, tile)
            for j, (_, d) in enumerate(mark):
                local = ids - (me_dev ^ d) * rows
                hot_ref[j * rows : (j + 1) * rows, tile * width : (tile + 1) * width] = jnp.where(
                    place == local, 1.0, 0.0
                ).astype(jnp.bfloat16)
        block = ref[...]
        gram = gram + lax.dot_general(block, block, side, preferred_element_type=jnp.float32)
        hot = hot_ref[: len(mark) * rows, :]
        found = lax.dot_general(
            block, hot, (((axis,), (0,)), ((), ())), preferred_element_type=jnp.float32
        )
        for tile in range(tiles):
            part = found[:, tile * width : (tile + 1) * width]
            at = g * tiles + tile
            rows_ref[at] = rows_ref[at] + part if g in seen else part
        seen.add(g)
    high, low = split(gram)
    gram_ref[:rank, :] = high
    gram_ref[rank:, :] = low

    def fold(value):
        if pack == 1:
            return value
        return value + pltpu.roll(value, users, 1)

    def image_of(vector):
        both = jnp.concatenate(split(vector), axis=1)
        image = jnp.dot(gram_ref[...], both, preferred_element_type=jnp.float32)
        image = image[:rank] + image[rank:]
        return image[:, :width] + image[:, width:] + RIDGE * vector

    def along(vector, at):
        return jnp.sum(rows_ref[at] * vector, axis=0, keepdims=True)

    x = start_ref[...].T
    if pack > 1:
        x = jnp.concatenate([x] * pack, axis=1)
    extra = jnp.zeros_like(x)
    for at in range(groups * tiles):
        extra = extra + (gains[at] - weights[at] * along(x, at)) * rows_ref[at]
    resid = fold(extra) - image_of(x)
    direction = resid
    norm_now = jnp.sum(resid * resid, axis=0, keepdims=True)
    for step in range(CG_STEPS):
        extra = jnp.zeros_like(x)
        for at in range(groups * tiles):
            extra = extra + (weights[at] * along(direction, at)) * rows_ref[at]
        image = fold(extra) + image_of(direction)
        alpha = norm_now / jnp.sum(direction * image, axis=0, keepdims=True)
        x = x + alpha * direction
        if step + 1 < CG_STEPS:
            resid = resid - alpha * image
            norm_next = jnp.sum(resid * resid, axis=0, keepdims=True)
            direction = resid + (norm_next / norm_now) * direction
            norm_now = norm_next
    x = x[:, :users]
    packed_ref[...] = x.astype(jnp.bfloat16)
    out_ref[...] = x.T


def half_step(start_x, own, axis, slot_ids, confidence, slot_mask):
    users, rank = start_x.shape
    rows = own.shape[axis]
    groups = slot_ids.shape[1]
    pieces = gather_pieces(own, axis)
    most = max(len(m) for _, m in pieces) * rows
    lanes = slot_ids.shape[2] * users
    vmem = pl.BlockSpec(memory_space=pltpu.VMEM)
    table = sum(p.size for p, _ in pieces) * 2
    return pl.pallas_call(
        functools.partial(solve_kernel, [m for _, m in pieces], axis, rows, groups),
        out_shape=(
            jax.ShapeDtypeStruct((users, rank), jnp.float32),
            jax.ShapeDtypeStruct((rank, users), jnp.bfloat16),
        ),
        in_specs=[vmem] * (4 + len(pieces)),
        out_specs=(vmem, vmem),
        scratch_shapes=[
            pltpu.VMEM((most, lanes), jnp.bfloat16),
            pltpu.VMEM((groups * lanes // max(users, LANES), rank, max(users, LANES)), jnp.float32),
            pltpu.VMEM((2 * rank, rank), jnp.bfloat16),
        ],
        compiler_params=pltpu.CompilerParams(
            vmem_limit_bytes=(16 if table <= 4 * MIB else 60) * MIB
        ),
    )(
        start_x,
        slot_ids.transpose(2, 1, 0),
        confidence.transpose(2, 1, 0),
        slot_mask.transpose(2, 1, 0),
        *[p for p, _ in pieces],
    )


def per_device(
    user_factors, item_factors, user_items, user_conf, user_mask, item_users, item_conf, item_mask
):
    packed = item_factors.astype(jnp.bfloat16)
    new_users, packed = half_step(user_factors, packed, 0, user_items, user_conf, user_mask)
    new_items, _ = half_step(item_factors, packed, 1, item_users, item_conf, item_mask)
    return (new_users, new_items)


def solution(mesh):
    rows2 = P(("grp", "dev"), None)
    rows3 = P(("grp", "dev"), None, None)
    return jax.shard_map(
        per_device,
        mesh=mesh,
        in_specs=(rows2, rows2) + (rows3,) * 6,
        out_specs=(rows2, rows2),
        check_vma=False,
    )
```

time: 81.7 us -> 59.6 us (0.73)
  Pallas kernels: 22 us -> 8.29 us
  local copies, waits for them, and re-layouts: 6.77 us -> 0.18 us
  starting transfers between devices: 22.2 us -> 20.1 us
  waiting for transfers between devices: 27.8 us -> 29.2 us
  other arithmetic: 1.78 us -> 0.93 us
    pallas_call x2, Pallas kernels: 22 us -> 8.29 us  [half_step(): pl.pallas_call(functools.partial(solve_kernel, [m for _, m in pieces], ax...]
    reshape x10 -> x0, local copies, waits for them, and re-layouts: 4.52 us -> none  [the longest x2 1.6 us: half_step(): slot_ids.reshape(-1)]
    ppermute x14 -> x16, starting transfers between devices: 22.2 us -> 20.1 us  [swap(): return lax.ppermute(value, axis, [(i, i ^ bit) for i in range(size)])]
    unnamed x38 -> x22, local copies, waits for them, and re-layouts: 2.19 us -> 0.1 us
    ppermute x14 -> x16, waiting for transfers between devices: 27.8 us -> 29.2 us  [swap(): return lax.ppermute(value, axis, [(i, i ^ bit) for i in range(size)])]
    concatenate x8 -> x6, other arithmetic: 0.94 us -> 0.09 us  [gather_pieces(): block = jnp.concatenate([block, swap(block, 'dev', bit)], axis=axis)]
  transfers between devices with their start and end apart: 14 -> 16, of which waited for: 12 -> 11; matrix products, arithmetic and copies ran while one was open for 6% -> 0% of each run, Pallas kernels for 0% -> 0%
where the time goes in v2:
time: 59.6 us; the launch traced here: 59.5 us
  waiting for transfers between devices  29.2 us (49%)
  starting transfers between devices  20.1 us (34%)
  Pallas kernels  8.29 us (14%)
  other arithmetic  0.93 us (2%)
  between operations  0.81 us (1%)
    ppermute x16, waiting for transfers between devices, swap(): return lax.ppermute(value, axis, [(i, i ^ bit) for i in range(size)])  29.2 us
    ppermute x16, starting transfers between devices, swap(): return lax.ppermute(value, axis, [(i, i ^ bit) for i in range(size)])  20.1 us
    pallas_call x2, Pallas kernels, half_step(): pl.pallas_call(functools.partial(solve_kernel, [m for _, m in pieces], ax...  8.29 us
  transfers between devices with their start and end apart: 16, of which 11 were waited for; matrix products, arithmetic and copies ran while one was open for 0% of the time, Pallas kernels for 0%

profile of v2, /device:TPU:0, one launch (start us, length us, event | category | flops | bytes accessed | tf_op | source)
XLA Modules:
  0.0 59.5 jit_solution(6601801561374068904)
XLA Ops:
  0.6 0.8 %convert_element_type.3 = bf16[64,256]{1,0:T(8,128)(2,1)S(1)} convert(f32[64,256]{1,0:T(8,128)} %refs_0_.3) | non-fusion elementwise | flops 16384 | bytes 98304 | tf_op jit(solution)/shard_map/convert_element_type | solution.py:187
  1.5 4.1 %collective-permute-start = (bf16[64,256]{1,0:T(8,128)(2,1)S(1)}, bf16[64,256]{1,0:T(8,128)(2,1)S(1)}, u32[]{:S(2)}, u32[]{:S(2)}) collective-permute-start(bf16[64,256]{1,0:T(8,128)(2,1)S(1)} %convert_element_type.3), channel_id=1, source_target_pairs={{0,8},{1,9},{2,10},{3,11},{4,12},{5,13},{6,14},{7,15},{8,0},{9,1},... | collective-permute-start | bytes 98312 | tf_op jit(solution)/shard_map/ppermute | solution.py:18
  5.5 2.2 %collective-permute-done = bf16[64,256]{1,0:T(8,128)(2,1)S(1)} collective-permute-done((bf16[64,256]{1,0:T(8,128)(2,1)S(1)}, bf16[64,256]{1,0:T(8,128)(2,1)S(1)}, u32[]{:S(2)}, u32[]{:S(2)}) %collective-permute-start) | collective-permute-done | bytes 32800 | tf_op jit(solution)/shard_map/ppermute | solution.py:18
  7.8 1.7 %collective-permute-start.1 = (bf16[128,256]{1,0:T(8,128)(2,1)S(1)}, bf16[128,256]{1,0:T(8,128)(2,1)S(1)}, u32[]{:S(2)}, u32[]{:S(2)}) collective-permute-start(bf16[128,256]{1,0:T(8,128)(2,1)S(1)} %pad_maximum_fusion.5), channel_id=1, source_target_pairs={{0,1},{1,0},{2,3},{3,2},{4,5},{5,4},{6,7},{7,6},{8,9},{9,8},{10,11... | collective-permute-start | bytes 196616 | tf_op jit(solution)/shard_map/ppermute | solution.py:18
  9.5 1.3 %collective-permute-start.3 = (bf16[128,256]{1,0:T(8,128)(2,1)S(1)}, bf16[128,256]{1,0:T(8,128)(2,1)S(1)}, u32[]{:S(2)}, u32[]{:S(2)}) collective-permute-start(bf16[128,256]{1,0:T(8,128)(2,1)S(1)} %pad_maximum_fusion.5), channel_id=1, source_target_pairs={{0,4},{1,5},{2,6},{3,7},{4,0},{5,1},{6,2},{7,3},{8,12},{9,13},{10,... | collective-permute-start | bytes 196616 | tf_op jit(solution)/shard_map/ppermute | solution.py:18
  10.8 1.2 %collective-permute-done.1 = bf16[128,256]{1,0:T(8,128)(2,1)S(1)} collective-permute-done((bf16[128,256]{1,0:T(8,128)(2,1)S(1)}, bf16[128,256]{1,0:T(8,128)(2,1)S(1)}, u32[]{:S(2)}, u32[]{:S(2)}) %collective-permute-start.1) | collective-permute-done | bytes 65568 | tf_op jit(solution)/shard_map/ppermute | solution.py:18
  12.1 1.8 %collective-permute-start.2 = (bf16[256,256]{1,0:T(8,128)(2,1)S(1)}, bf16[256,256]{1,0:T(8,128)(2,1)S(1)}, u32[]{:S(2)}, u32[]{:S(2)}) collective-permute-start(bf16[256,256]{1,0:T(8,128)(2,1)S(1)} %pad_maximum_fusion.3), channel_id=1, source_target_pairs={{0,2},{1,3},{2,0},{3,1},{4,6},{5,7},{6,4},{7,5},{8,10},{9,11},{10,... | collective-permute-start | bytes 393224 | tf_op jit(solution)/shard_map/ppermute | solution.py:18
  13.9 0.0 collective-permute-done.3
  13.9 1.4 %collective-permute-start.4 = (bf16[128,256]{1,0:T(8,128)(2,1)S(1)}, bf16[128,256]{1,0:T(8,128)(2,1)S(1)}, u32[]{:S(2)}, u32[]{:S(2)}) collective-permute-start(bf16[128,256]{1,0:T(8,128)(2,1)S(1)} %collective-permute-done.3), channel_id=1, source_target_pairs={{0,2},{1,3},{2,0},{3,1},{4,6},{5,7},{6,4},{7,5},{8,10},{9,11},{10,... | collective-permute-start | bytes 196616 | tf_op jit(solution)/shard_map/ppermute | solution.py:18
  15.3 2.9 %collective-permute-done.4 = bf16[128,256]{1,0:T(8,128)(2,1)S(1)} collective-permute-done((bf16[128,256]{1,0:T(8,128)(2,1)S(1)}, bf16[128,256]{1,0:T(8,128)(2,1)S(1)}, u32[]{:S(2)}, u32[]{:S(2)}) %collective-permute-start.4) | collective-permute-done | bytes 65568 | tf_op jit(solution)/shard_map/ppermute | solution.py:18
  18.1 1.6 %collective-permute-start.5 = (bf16[256,256]{1,0:T(8,128)(2,1)S(1)}, bf16[256,256]{1,0:T(8,128)(2,1)S(1)}, u32[]{:S(2)}, u32[]{:S(2)}) collective-permute-start(bf16[256,256]{1,0:T(8,128)(2,1)S(1)} %pad_maximum_fusion.4), channel_id=1, source_target_pairs={{0,1},{1,0},{2,3},{3,2},{4,5},{5,4},{6,7},{7,6},{8,9},{9,8},{10,11... | collective-permute-start | bytes 393224 | tf_op jit(solution)/shard_map/ppermute | solution.py:18
  19.7 0.0 collective-permute-done.2
  19.7 0.0 copy-start.1
  19.8 0.1 collective-permute-start.6
  19.8 3.3 %collective-permute-done.5 = bf16[256,256]{1,0:T(8,128)(2,1)S(1)} collective-permute-done((bf16[256,256]{1,0:T(8,128)(2,1)S(1)}, bf16[256,256]{1,0:T(8,128)(2,1)S(1)}, u32[]{:S(2)}, u32[]{:S(2)}) %collective-permute-start.5) | collective-permute-done | bytes 131104 | tf_op jit(solution)/shard_map/ppermute | solution.py:18
  23.2 0.0 copy-start.6
  23.2 0.0 copy-start.7
  23.2 0.0 copy-start.5
  23.2 0.1 collective-permute-start.7
  23.3 0.0 collective-permute-done.6.refs_6_
  23.3 1.5 %collective-permute-done.7.refs_7_ = bf16[512,256]{1,0:T(8,128)(2,1)S(1)} collective-permute-done((bf16[512,256]{1,0:T(8,128)(2,1)S(1)}, bf16[512,256]{1,0:T(8,128)(2,1)S(1)}, u32[]{:S(2)}, u32[]{:S(2)}) %collective-permute-start.7) | collective-permute-done | bytes 262176 | tf_op jit(solution)/shard_map/ppermute | solution.py:18
  24.8 0.0 copy-done.1
  24.8 0.0 copy-done.6
  24.8 0.0 copy-done.7
  24.8 0.0 copy-done.5
  24.8 3.6 %shard_map.95 = (f32[128,256]{1,0:T(8,128)}, bf16[256,128]{1,0:T(8,128)(2,1)S(1)}) custom-call(f32[128,256]{1,0:T(8,128)S(1)} %copy-done.1, s32[3,2,128]{2,1,0:T(2,128)S(1)} %bitcast.9, f32[3,2,128]{2,1,0:T(2,128)S(1)} %bitcast.10, s32[3,2,128]{2,1,0:T(2,128)S(1)} %bitcast.11, bf16[512,256]{1,0:T(8,128)(2,1)S(1)} %pad_maximum_fusion.refs_4_, ...), custom_call_target="tpu_custom_call" | custom-call | tf_op jit(solution)/shard_map/pallas_call | solution.py:159
  28.5 2.4 %collective-permute-start.8 = (bf16[256,128]{1,0:T(8,128)(2,1)S(1)}, bf16[256,128]{1,0:T(8,128)(2,1)S(1)}, u32[]{:S(2)}, u32[]{:S(2)}) collective-permute-start(bf16[256,128]{1,0:T(8,128)(2,1)S(1)} %get-tuple-element.6), channel_id=1, source_target_pairs={{0,8},{1,9},{2,10},{3,11},{4,12},{5,13},{6,14},{7,15},{8,0},{9,1},... | collective-permute-start | bytes 196616 | tf_op jit(solution)/shard_map/ppermute | solution.py:18
  30.9 4.2 %collective-permute-done.8 = bf16[256,128]{1,0:T(8,128)(2,1)S(1)} collective-permute-done((bf16[256,128]{1,0:T(8,128)(2,1)S(1)}, bf16[256,128]{1,0:T(8,128)(2,1)S(1)}, u32[]{:S(2)}, u32[]{:S(2)}) %collective-permute-start.8) | collective-permute-done | bytes 65568 | tf_op jit(solution)/shard_map/ppermute | solution.py:18
  35.1 0.4 collective-permute-start.11
  35.5 1.5 %collective-permute-start.9 = (bf16[256,256]{1,0:T(8,128)(2,1)S(1)}, bf16[256,256]{1,0:T(8,128)(2,1)S(1)}, u32[]{:S(2)}, u32[]{:S(2)}) collective-permute-start(bf16[256,256]{1,0:T(8,128)(2,1)S(1)} %get-tuple-element.8), channel_id=1, source_target_pairs={{0,1},{1,0},{2,3},{3,2},{4,5},{5,4},{6,7},{7,6},{8,9},{9,8},{10,11... | collective-permute-start | bytes 393224 | tf_op jit(solution)/shard_map/ppermute | solution.py:18
  36.9 3.2 %collective-permute-done.11 = bf16[256,256]{1,0:T(8,128)(2,1)S(1)} collective-permute-done((bf16[256,256]{1,0:T(8,128)(2,1)S(1)}, bf16[256,256]{1,0:T(8,128)(2,1)S(1)}, u32[]{:S(2)}, u32[]{:S(2)}) %collective-permute-start.11) | collective-permute-done | bytes 131104 | tf_op jit(solution)/shard_map/ppermute | solution.py:18
  40.1 1.4 %collective-permute-start.12 = (bf16[256,256]{1,0:T(8,128)(2,1)S(1)}, bf16[256,256]{1,0:T(8,128)(2,1)S(1)}, u32[]{:S(2)}, u32[]{:S(2)}) collective-permute-start(bf16[256,256]{1,0:T(8,128)(2,1)S(1)} %collective-permute-done.11), channel_id=1, source_target_pairs={{0,2},{1,3},{2,0},{3,1},{4,6},{5,7},{6,4},{7,5},{8,10},{9,11},{10,... | collective-permute-start | bytes 393224 | tf_op jit(solution)/shard_map/ppermute | solution.py:18
  41.5 0.0 collective-permute-done.9
  41.5 0.7 %collective-permute-start.10 = (bf16[256,512]{1,0:T(8,128)(2,1)S(1)}, bf16[256,512]{1,0:T(8,128)(2,1)S(1)}, u32[]{:S(2)}, u32[]{:S(2)}) collective-permute-start(bf16[256,512]{1,0:T(8,128)(2,1)S(1)} %pad_maximum_fusion.1), channel_id=1, source_target_pairs={{0,2},{1,3},{2,0},{3,1},{4,6},{5,7},{6,4},{7,5},{8,10},{9,11},{10,... | collective-permute-start | bytes 786440 | tf_op jit(solution)/shard_map/ppermute | solution.py:18
  42.2 4.1 %collective-permute-done.12 = bf16[256,256]{1,0:T(8,128)(2,1)S(1)} collective-permute-done((bf16[256,256]{1,0:T(8,128)(2,1)S(1)}, bf16[256,256]{1,0:T(8,128)(2,1)S(1)}, u32[]{:S(2)}, u32[]{:S(2)}) %collective-permute-start.12) | collective-permute-done | bytes 131104 | tf_op jit(solution)/shard_map/ppermute | solution.py:18
  46.3 1.6 %collective-permute-start.13 = (bf16[256,512]{1,0:T(8,128)(2,1)S(1)}, bf16[256,512]{1,0:T(8,128)(2,1)S(1)}, u32[]{:S(2)}, u32[]{:S(2)}) collective-permute-start(bf16[256,512]{1,0:T(8,128)(2,1)S(1)} %pad_maximum_fusion.2), channel_id=1, source_target_pairs={{0,1},{1,0},{2,3},{3,2},{4,5},{5,4},{6,7},{7,6},{8,9},{9,8},{10,11... | collective-permute-start | bytes 786440 | tf_op jit(solution)/shard_map/ppermute | solution.py:18
  47.9 1.2 %collective-permute-done.10 = bf16[256,512]{1,0:T(8,128)(2,1)S(1)} collective-permute-done((bf16[256,512]{1,0:T(8,128)(2,1)S(1)}, bf16[256,512]{1,0:T(8,128)(2,1)S(1)}, u32[]{:S(2)}, u32[]{:S(2)}) %collective-permute-start.10) | collective-permute-done | bytes 262176 | tf_op jit(solution)/shard_map/ppermute | solution.py:18
  49.1 0.0 copy-start
  49.2 0.1 collective-permute-start.14
  49.2 3.5 %collective-permute-done.13 = bf16[256,512]{1,0:T(8,128)(2,1)S(1)} collective-permute-done((bf16[256,512]{1,0:T(8,128)(2,1)S(1)}, bf16[256,512]{1,0:T(8,128)(2,1)S(1)}, u32[]{:S(2)}, u32[]{:S(2)}) %collective-permute-start.13) | collective-permute-done | bytes 262176 | tf_op jit(solution)/shard_map/ppermute | solution.py:18
  52.8 0.0 copy-start.2
  52.8 0.0 copy-start.3
  52.8 0.0 copy-start.4
  52.8 0.1 collective-permute-start.15
  52.9 0.0 collective-permute-done.14.refs_6_
  52.9 1.9 %collective-permute-done.15.refs_7_ = bf16[256,1024]{1,0:T(8,128)(2,1)S(1)} collective-permute-done((bf16[256,1024]{1,0:T(8,128)(2,1)S(1)}, bf16[256,1024]{1,0:T(8,128)(2,1)S(1)}, u32[]{:S(2)}, u32[]{:S(2)}) %collective-permute-start.15) | collective-permute-done | bytes 524320 | tf_op jit(solution)/shard_map/ppermute | solution.py:18
  54.8 0.0 copy-done
  54.8 0.0 copy-done.2
  54.8 0.0 copy-done.3
  54.8 0.0 copy-done.4
  54.8 4.7 %shard_map.96 = (f32[64,256]{1,0:T(8,128)}, bf16[256,64]{1,0:T(8,128)(2,1)}) custom-call(f32[64,256]{1,0:T(8,128)S(1)} %copy-done, s32[6,2,64]{2,1,0:T(2,128)S(1)} %bitcast.6, f32[6,2,64]{2,1,0:T(2,128)S(1)} %bitcast.7, s32[6,2,64]{2,1,0:T(2,128)S(1)} %bitcast.8, bf16[256,1024]{1,0:T(8,128)(2,1)S(1)} %constant_dynamic-update-slice_fusion.5.refs_4_, ...), custom_call_target="tpu_custom_call" | custom-call | tf_op jit(solution)/shard_map/pallas_call | solution.py:159
  (16 shorter events, 0.2 us)
Async XLA Ops:
  1.5 6.3 %collective-permute-start = (bf16[64,256]{1,0:T(8,128)(2,1)S(1)}, bf16[64,256]{1,0:T(8,128)(2,1)S(1)}, u32[]{:S(2)}, u32[]{:S(2)}) collective-permute-start(bf16[64,256]{1,0:T(8,128)(2,1)S(1)} %convert_element_type.3), channel_id=1, source_target_pairs={{0,8},{1,9},{2,10},{3,11},{4,12},{5,13},{6,14},{7,15},{8,0},{9,1},... | collective-permute-start | bytes 98312 | tf_op jit(solution)/shard_map/ppermute | solution.py:18
  7.8 4.3 %collective-permute-start.1 = (bf16[128,256]{1,0:T(8,128)(2,1)S(1)}, bf16[128,256]{1,0:T(8,128)(2,1)S(1)}, u32[]{:S(2)}, u32[]{:S(2)}) collective-permute-start(bf16[128,256]{1,0:T(8,128)(2,1)S(1)} %pad_maximum_fusion.5), channel_id=1, source_target_pairs={{0,1},{1,0},{2,3},{3,2},{4,5},{5,4},{6,7},{7,6},{8,9},{9,8},{10,11... | collective-permute-start | bytes 196616 | tf_op jit(solution)/shard_map/ppermute | solution.py:18
  9.5 4.4 %collective-permute-start.3 = (bf16[128,256]{1,0:T(8,128)(2,1)S(1)}, bf16[128,256]{1,0:T(8,128)(2,1)S(1)}, u32[]{:S(2)}, u32[]{:S(2)}) collective-permute-start(bf16[128,256]{1,0:T(8,128)(2,1)S(1)} %pad_maximum_fusion.5), channel_id=1, source_target_pairs={{0,4},{1,5},{2,6},{3,7},{4,0},{5,1},{6,2},{7,3},{8,12},{9,13},{10,... | collective-permute-start | bytes 196616 | tf_op jit(solution)/shard_map/ppermute | solution.py:18
  12.1 7.6 %collective-permute-start.2 = (bf16[256,256]{1,0:T(8,128)(2,1)S(1)}, bf16[256,256]{1,0:T(8,128)(2,1)S(1)}, u32[]{:S(2)}, u32[]{:S(2)}) collective-permute-start(bf16[256,256]{1,0:T(8,128)(2,1)S(1)} %pad_maximum_fusion.3), channel_id=1, source_target_pairs={{0,2},{1,3},{2,0},{3,1},{4,6},{5,7},{6,4},{7,5},{8,10},{9,11},{10,... | collective-permute-start | bytes 393224 | tf_op jit(solution)/shard_map/ppermute | solution.py:18
  13.9 4.3 %collective-permute-start.4 = (bf16[128,256]{1,0:T(8,128)(2,1)S(1)}, bf16[128,256]{1,0:T(8,128)(2,1)S(1)}, u32[]{:S(2)}, u32[]{:S(2)}) collective-permute-start(bf16[128,256]{1,0:T(8,128)(2,1)S(1)} %collective-permute-done.3), channel_id=1, source_target_pairs={{0,2},{1,3},{2,0},{3,1},{4,6},{5,7},{6,4},{7,5},{8,10},{9,11},{10,... | collective-permute-start | bytes 196616 | tf_op jit(solution)/shard_map/ppermute | solution.py:18
  18.1 5.0 %collective-permute-start.5 = (bf16[256,256]{1,0:T(8,128)(2,1)S(1)}, bf16[256,256]{1,0:T(8,128)(2,1)S(1)}, u32[]{:S(2)}, u32[]{:S(2)}) collective-permute-start(bf16[256,256]{1,0:T(8,128)(2,1)S(1)} %pad_maximum_fusion.4), channel_id=1, source_target_pairs={{0,1},{1,0},{2,3},{3,2},{4,5},{5,4},{6,7},{7,6},{8,9},{9,8},{10,11... | collective-permute-start | bytes 393224 | tf_op jit(solution)/shard_map/ppermute | solution.py:18
  19.7 5.1 %copy-start.1 = (f32[128,256]{1,0:T(8,128)S(1)}, f32[128,256]{1,0:T(8,128)}, u32[]{:S(2)}) copy-start(f32[128,256]{1,0:T(8,128)} %refs_0_.2) | copy-start | bytes 393220
  19.8 3.5 %collective-permute-start.6 = (bf16[512,256]{1,0:T(8,128)(2,1)S(1)}, bf16[512,256]{1,0:T(8,128)(2,1)S(1)}, u32[]{:S(2)}, u32[]{:S(2)}) collective-permute-start(bf16[512,256]{1,0:T(8,128)(2,1)S(1)} %pad_maximum_fusion.refs_4_), channel_id=1, source_target_pairs={{0,16},{16,0},{1,17},{17,1},{2,18},{18,2},{3,19},{19,3},{4,20},{20... | collective-permute-start | bytes 786440 | tf_op jit(solution)/shard_map/ppermute | solution.py:18
  23.2 1.6 %copy-start.6 = (f32[128,2,3]{0,1,2:T(2,128)S(1)}, f32[128,2,3]{0,1,2:T(2,128)}, u32[]{:S(2)}) copy-start(f32[128,2,3]{0,1,2:T(2,128)} %param.11) | copy-start | bytes 9220
  23.2 1.6 %copy-start.7 = (s32[128,2,3]{0,1,2:T(2,128)S(1)}, s32[128,2,3]{0,1,2:T(2,128)}, u32[]{:S(2)}) copy-start(s32[128,2,3]{0,1,2:T(2,128)} %param.12) | copy-start | bytes 9220
  23.2 1.6 %copy-start.5 = (s32[128,2,3]{0,1,2:T(2,128)S(1)}, s32[128,2,3]{0,1,2:T(2,128)}, u32[]{:S(2)}) copy-start(s32[128,2,3]{0,1,2:T(2,128)} %param.10) | copy-start | bytes 9220
  23.2 1.6 %collective-permute-start.7 = (bf16[512,256]{1,0:T(8,128)(2,1)S(1)}, bf16[512,256]{1,0:T(8,128)(2,1)S(1)}, u32[]{:S(2)}, u32[]{:S(2)}) collective-permute-start(bf16[512,256]{1,0:T(8,128)(2,1)S(1)} %constant_dynamic-update-slice_fusion.refs_5_), channel_id=1, source_target_pairs={{0,16},{16,0},{1,17},{17,1},{2,18},{18,2},{3,19},{19,3},{4,20},{20... | collective-permute-start | bytes 786440 | tf_op jit(solution)/shard_map/ppermute | solution.py:18
  28.5 6.6 %collective-permute-start.8 = (bf16[256,128]{1,0:T(8,128)(2,1)S(1)}, bf16[256,128]{1,0:T(8,128)(2,1)S(1)}, u32[]{:S(2)}, u32[]{:S(2)}) collective-permute-start(bf16[256,128]{1,0:T(8,128)(2,1)S(1)} %get-tuple-element.6), channel_id=1, source_target_pairs={{0,8},{1,9},{2,10},{3,11},{4,12},{5,13},{6,14},{7,15},{8,0},{9,1},... | collective-permute-start | bytes 196616 | tf_op jit(solution)/shard_map/ppermute | solution.py:18
  35.1 5.0 %collective-permute-start.11 = (bf16[256,256]{1,0:T(8,128)(2,1)S(1)}, bf16[256,256]{1,0:T(8,128)(2,1)S(1)}, u32[]{:S(2)}, u32[]{:S(2)}) collective-permute-start(bf16[256,256]{1,0:T(8,128)(2,1)S(1)} %get-tuple-element.8), channel_id=1, source_target_pairs={{0,4},{1,5},{2,6},{3,7},{4,0},{5,1},{6,2},{7,3},{8,12},{9,13},{10,... | collective-permute-start | bytes 393224 | tf_op jit(solution)/shard_map/ppermute | solution.py:18
  35.5 6.1 %collective-permute-start.9 = (bf16[256,256]{1,0:T(8,128)(2,1)S(1)}, bf16[256,256]{1,0:T(8,128)(2,1)S(1)}, u32[]{:S(2)}, u32[]{:S(2)}) collective-permute-start(bf16[256,256]{1,0:T(8,128)(2,1)S(1)} %get-tuple-element.8), channel_id=1, source_target_pairs={{0,1},{1,0},{2,3},{3,2},{4,5},{5,4},{6,7},{7,6},{8,9},{9,8},{10,11... | collective-permute-start | bytes 393224 | tf_op jit(solution)/shard_map/ppermute | solution.py:18
  40.1 6.2 %collective-permute-start.12 = (bf16[256,256]{1,0:T(8,128)(2,1)S(1)}, bf16[256,256]{1,0:T(8,128)(2,1)S(1)}, u32[]{:S(2)}, u32[]{:S(2)}) collective-permute-start(bf16[256,256]{1,0:T(8,128)(2,1)S(1)} %collective-permute-done.11), channel_id=1, source_target_pairs={{0,2},{1,3},{2,0},{3,1},{4,6},{5,7},{6,4},{7,5},{8,10},{9,11},{10,... | collective-permute-start | bytes 393224 | tf_op jit(solution)/shard_map/ppermute | solution.py:18
  41.5 7.6 %collective-permute-start.10 = (bf16[256,512]{1,0:T(8,128)(2,1)S(1)}, bf16[256,512]{1,0:T(8,128)(2,1)S(1)}, u32[]{:S(2)}, u32[]{:S(2)}) collective-permute-start(bf16[256,512]{1,0:T(8,128)(2,1)S(1)} %pad_maximum_fusion.1), channel_id=1, source_target_pairs={{0,2},{1,3},{2,0},{3,1},{4,6},{5,7},{6,4},{7,5},{8,10},{9,11},{10,... | collective-permute-start | bytes 786440 | tf_op jit(solution)/shard_map/ppermute | solution.py:18
  46.3 6.4 %collective-permute-start.13 = (bf16[256,512]{1,0:T(8,128)(2,1)S(1)}, bf16[256,512]{1,0:T(8,128)(2,1)S(1)}, u32[]{:S(2)}, u32[]{:S(2)}) collective-permute-start(bf16[256,512]{1,0:T(8,128)(2,1)S(1)} %pad_maximum_fusion.2), channel_id=1, source_target_pairs={{0,1},{1,0},{2,3},{3,2},{4,5},{5,4},{6,7},{7,6},{8,9},{9,8},{10,11... | collective-permute-start | bytes 786440 | tf_op jit(solution)/shard_map/ppermute | solution.py:18
  49.1 5.6 %copy-start = (f32[64,256]{1,0:T(8,128)S(1)}, f32[64,256]{1,0:T(8,128)}, u32[]{:S(2)}) copy-start(f32[64,256]{1,0:T(8,128)} %refs_0_.3) | copy-start | bytes 196612
  49.2 3.7 %collective-permute-start.14 = (bf16[256,1024]{1,0:T(8,128)(2,1)S(1)}, bf16[256,1024]{1,0:T(8,128)(2,1)S(1)}, u32[]{:S(2)}, u32[]{:S(2)}) collective-permute-start(bf16[256,1024]{1,0:T(8,128)(2,1)S(1)} %constant_dynamic-update-slice_fusion.5.refs_4_), channel_id=1, source_target_pairs={{0,16},{16,0},{1,17},{17,1},{2,18},{18,2},{3,19},{19,3},{4,20},{20... | collective-permute-start | bytes 1572872 | tf_op jit(solution)/shard_map/ppermute | solution.py:18
  52.8 2.0 %copy-start.2 = (s32[64,2,6]{0,1,2:T(2,128)S(1)}, s32[64,2,6]{0,1,2:T(2,128)}, u32[]{:S(2)}) copy-start(s32[64,2,6]{0,1,2:T(2,128)} %param.13) | copy-start | bytes 9220
  52.8 2.0 %copy-start.3 = (f32[64,2,6]{0,1,2:T(2,128)S(1)}, f32[64,2,6]{0,1,2:T(2,128)}, u32[]{:S(2)}) copy-start(f32[64,2,6]{0,1,2:T(2,128)} %param.14) | copy-start | bytes 9220
  52.8 2.0 %copy-start.4 = (s32[64,2,6]{0,1,2:T(2,128)S(1)}, s32[64,2,6]{0,1,2:T(2,128)}, u32[]{:S(2)}) copy-start(s32[64,2,6]{0,1,2:T(2,128)} %param.15) | copy-start | bytes 9220
  52.8 2.0 %collective-permute-start.15 = (bf16[256,1024]{1,0:T(8,128)(2,1)S(1)}, bf16[256,1024]{1,0:T(8,128)(2,1)S(1)}, u32[]{:S(2)}, u32[]{:S(2)}) collective-permute-start(bf16[256,1024]{1,0:T(8,128)(2,1)S(1)} %constant_dynamic-update-slice_fusion.9.refs_5_), channel_id=1, source_target_pairs={{0,16},{16,0},{1,17},{17,1},{2,18},{18,2},{3,19},{19,3},{4,20},{20... | collective-permute-start | bytes 1572872 | tf_op jit(solution)/shard_map/ppermute | solution.py:18

commit v3 on v2

v3 whole, which is shorter than its diff:
```python
import functools

import jax
import jax.numpy as jnp
from jax import lax
from jax.experimental import pallas as pl
from jax.experimental.pallas import tpu as pltpu
from jax.sharding import PartitionSpec as P


CG_STEPS = 4
RIDGE = 1.0
LANES = 128
SHORT = 48 * 1024
MIB = 1024 * 1024


def swap(value, axis, bit):
    size = lax.axis_size(axis)
    return lax.ppermute(value, axis, [(i, i ^ bit) for i in range(size)])


def bits_of(size):
    return [1 << b for b in range(size.bit_length() - 1)]


def gather_pieces(own, axis):
    first, second, near, *far = bits_of(lax.axis_size("dev"))

    def move(piece, bit):
        block, marks = piece
        return swap(block, "dev", bit), [o ^ bit for o in marks]

    def join(pieces):
        return jnp.concatenate([b for b, _ in pieces], axis=axis), sum((m for _, m in pieces), [])

    def mine(piece):
        return piece[0], [(0, o) for o in piece[1]]

    def spread(piece):
        group = [mine(piece)]
        for bit in bits_of(lax.axis_size("grp")):
            group = group + [(swap(b, "grp", bit), [(g ^ bit, o) for g, o in m]) for b, m in group]
        return group

    a = (own, [0])
    if own.size * 2 <= SHORT:
        for bit in far[::-1]:
            a = join([a, move(a, bit)])
        b = move(a, near)
        ax, ay = move(a, first), move(a, second)
        bx = move(b, first)
        more = move(join([ax, b]), second)
        last = move(bx, second)
        one = spread(join([a, b, ax, ay, bx]))
        two = spread(join([more, last]))
        return one, [mine(more)], [mine(last)], two[1:]
    b = None
    for bit in far[::-1]:
        moved = move(a, bit)
        if b is None:
            b = move(a, near)
        b = join([b, move(moved, near)])
        a = join([a, moved])
    ax, ay = move(a, first), move(a, second)
    bx, by = move(b, first), move(b, second)
    axy = move(ay, first)
    bxy = move(bx, second)
    one = spread(join([a, b, ax, ay]))
    two = spread(join([bx, by, axy]))
    three = spread(bxy)
    return one, two, three[:1], three[1:]


def split(value):
    high = value.astype(jnp.bfloat16)
    low = (value - high.astype(jnp.float32)).astype(jnp.bfloat16)
    return high, low


def shape_of(ids_ref, users):
    pack = max(1, LANES // users)
    return pack, pack * users, ids_ref.shape[0] // pack


def row_of(ref, g, tile, pack):
    block = lax.axis_index("grp") ^ g
    parts = [ref[tile * pack + i, pl.ds(block, 1), :] for i in range(pack)]
    return parts[0] if pack == 1 else jnp.concatenate(parts, axis=1)


def absorb(marks, axis, rows, users, ids_ref, piece_refs, hot_ref, gram, table_ref, seen):
    pack, width, tiles = shape_of(ids_ref, users)
    me_dev = lax.axis_index("dev")
    side = (((axis,), (axis,)), ((), ()))
    place = lax.broadcasted_iota(jnp.int32, (rows, width), 0)
    for ref, mark in zip(piece_refs, marks):
        g = mark[0][0]
        for tile in range(tiles):
            ids = row_of(ids_ref, g, tile, pack)
            for j, (_, d) in enumerate(mark):
                local = ids - (me_dev ^ d) * rows
                hot_ref[j * rows : (j + 1) * rows, tile * width : (tile + 1) * width] = jnp.where(
                    place == local, 1.0, 0.0
                ).astype(jnp.bfloat16)
        block = ref[...]
        part = lax.dot_general(block, block, side, preferred_element_type=jnp.float32)
        gram = part if gram is None else gram + part
        hot = hot_ref[: len(mark) * rows, :]
        found = lax.dot_general(
            block, hot, (((axis,), (0,)), ((), ())), preferred_element_type=jnp.float32
        )
        for tile in range(tiles):
            part = found[:, tile * width : (tile + 1) * width]
            at = g * tiles + tile
            table_ref[at] = table_ref[at] + part if g in seen else part
        seen.add(g)
    return gram


def early_kernel(marks, axis, rows, *refs, groups):
    count = len(marks)
    ids_ref, conf_ref, mask_ref, start_ref = refs[:4]
    piece_refs = refs[4 : 4 + count]
    gram_out, table_out, x_out, weight_out, gain_out, hot_ref = refs[4 + count :]
    users = start_ref.shape[0]
    pack, _, tiles = shape_of(ids_ref, users)
    for g in range(groups):
        for tile in range(tiles):
            at = g * tiles + tile
            mask = row_of(mask_ref, g, tile, pack).astype(jnp.float32)
            weight = row_of(conf_ref, g, tile, pack) * mask
            weight_out[at : at + 1, :] = weight
            gain_out[at : at + 1, :] = mask + weight
    x = start_ref[...].T
    x_out[...] = x if pack == 1 else jnp.concatenate([x] * pack, axis=1)
    gram_out[...] = absorb(
        marks, axis, rows, users, ids_ref, piece_refs, hot_ref, None, table_out, set()
    )


def own_kernel(marks, axis, rows, *refs, users):
    count = len(marks)
    ids_ref, gram_in, table_in = refs[:3]
    piece_refs = refs[3 : 3 + count]
    gram_out, table_out, hot_ref = refs[3 + count :]
    for at in range(table_in.shape[0]):
        table_out[at] = table_in[at]
    gram_out[...] = absorb(
        marks, axis, rows, users, ids_ref, piece_refs, hot_ref, gram_in[...], table_out,
        {m[0][0] for m in marks},
    )


def solve_kernel(marks, axis, rows, *refs, groups, users):
    count = len(marks)
    ids_ref, gram_in, table_ref, start_ref, weight_ref, gain_ref = refs[:6]
    piece_refs = refs[6 : 6 + count]
    out_ref, packed_ref, rows_ref, hot_ref, gram_ref = refs[6 + count :]
    rank = start_ref.shape[0]
    pack, width, tiles = shape_of(ids_ref, users)
    weights = [weight_ref[at : at + 1, :] for at in range(groups * tiles)]
    gains = [gain_ref[at : at + 1, :] for at in range(groups * tiles)]

    touched = {m[0][0] for m in marks}
    for at in range(groups * tiles):
        rows_ref[at] = table_ref[at]
    gram = absorb(
        marks, axis, rows, users, ids_ref, piece_refs, hot_ref, gram_in[...], rows_ref, touched
    )
    high, low = split(gram)
    gram_ref[:rank, :] = high
    gram_ref[rank:, :] = low

    def fold(value):
        if pack == 1:
            return value
        return value + pltpu.roll(value, users, 1)

    def image_of(vector):
        both = jnp.concatenate(split(vector), axis=1)
        image = jnp.dot(gram_ref[...], both, preferred_element_type=jnp.float32)
        image = image[:rank] + image[rank:]
        return image[:, :width] + image[:, width:] + RIDGE * vector

    def along(vector, at):
        return jnp.sum(rows_ref[at] * vector, axis=0, keepdims=True)

    x = start_ref[...]
    extra = jnp.zeros_like(x)
    for at in range(groups * tiles):
        extra = extra + (gains[at] - weights[at] * along(x, at)) * rows_ref[at]
    resid = fold(extra) - image_of(x)
    direction = resid
    norm_now = jnp.sum(resid * resid, axis=0, keepdims=True)
    for step in range(CG_STEPS):
        extra = jnp.zeros_like(x)
        for at in range(groups * tiles):
            extra = extra + (weights[at] * along(direction, at)) * rows_ref[at]
        image = fold(extra) + image_of(direction)
        alpha = norm_now / jnp.sum(direction * image, axis=0, keepdims=True)
        x = x + alpha * direction
        if step + 1 < CG_STEPS:
            resid = resid - alpha * image
            norm_next = jnp.sum(resid * resid, axis=0, keepdims=True)
            direction = resid + (norm_next / norm_now) * direction
            norm_now = norm_next
    x = x[:, :users]
    packed_ref[...] = x.astype(jnp.bfloat16)
    out_ref[...] = x if out_ref.shape == x.shape else x.T


def half_step(start_x, own, axis, slot_ids, confidence, slot_mask):
    users, rank = start_x.shape
    rows = own.shape[axis]
    groups, slots = slot_ids.shape[1:]
    first, second, third, fourth = gather_pieces(own, axis)
    ids = slot_ids.transpose(2, 1, 0)
    width = max(users, LANES)
    lanes = slots * users
    vmem = pl.BlockSpec(memory_space=pltpu.VMEM)
    small = lax.axis_size("dev") * groups * rows * rank <= 2 * MIB
    params = pltpu.CompilerParams(vmem_limit_bytes=(16 if small else 60) * MIB)
    gram_shape = jax.ShapeDtypeStruct((rank, rank), jnp.float32)
    table_shape = jax.ShapeDtypeStruct((groups * lanes // width, rank, width), jnp.float32)

    def hot_scratch(pieces):
        return pltpu.VMEM((max(len(m) for _, m in pieces) * rows, lanes), jnp.bfloat16)

    def cost(pieces):
        table = sum(p.size for p, _ in pieces)
        return pl.CostEstimate(
            flops=2 * table * (rank + lanes), bytes_accessed=2 * table, transcendentals=0
        )

    def call(kernel, pieces, operands, out_shape, scratch):
        return pl.pallas_call(
            functools.partial(kernel, [m for _, m in pieces], axis, rows),
            out_shape=out_shape,
            in_specs=[vmem] * (len(operands) + len(pieces)),
            out_specs=(vmem,) * len(out_shape),
            scratch_shapes=scratch,
            compiler_params=params,
            cost_estimate=cost(pieces),
        )(*operands, *[p for p, _ in pieces])

    tiles = table_shape.shape[0]
    line_shape = jax.ShapeDtypeStruct((tiles, width), jnp.float32)
    gram, table, start, weight, gain = call(
        functools.partial(early_kernel, groups=groups),
        first,
        (ids, confidence.transpose(2, 1, 0), slot_mask.transpose(2, 1, 0), start_x),
        (gram_shape, table_shape, jax.ShapeDtypeStruct((rank, width), jnp.float32), line_shape, line_shape),
        [hot_scratch(first)],
    )
    for pieces in (second, third):
        gram, table = call(
            functools.partial(own_kernel, users=users),
            pieces,
            (ids, gram, table),
            (gram_shape, table_shape),
            [hot_scratch(pieces)],
        )
    return call(
        functools.partial(solve_kernel, groups=groups, users=users),
        fourth,
        (ids, gram, table, start, weight, gain),
        (
            jax.ShapeDtypeStruct((rank, users) if axis == 0 else (users, rank), jnp.float32),
            jax.ShapeDtypeStruct((rank, users), jnp.bfloat16),
        ),
        [
            pltpu.VMEM(table_shape.shape, jnp.float32),
            hot_scratch(fourth),
            pltpu.VMEM((2 * rank, rank), jnp.bfloat16),
        ],
    )


def turn_kernel(value_ref, out_ref):
    out_ref[...] = value_ref[...].T


def turn(value):
    vmem = pl.BlockSpec(memory_space=pltpu.VMEM)
    return pl.pallas_call(
        turn_kernel,
        out_shape=jax.ShapeDtypeStruct(value.shape[::-1], value.dtype),
        in_specs=[vmem],
        out_specs=vmem,
        compiler_params=pltpu.CompilerParams(vmem_limit_bytes=8 * MIB),
        name="turn",
    )(value)


def per_device(
    user_factors, item_factors, user_items, user_conf, user_mask, item_users, item_conf, item_mask
):
    packed = item_factors.astype(jnp.bfloat16)
    new_users, packed = half_step(user_factors, packed, 0, user_items, user_conf, user_mask)
    new_users = turn(new_users)
    new_items, _ = half_step(item_factors, packed, 1, item_users, item_conf, item_mask)
    return (new_users, new_items)


def solution(mesh):
    rows2 = P(("grp", "dev"), None)
    rows3 = P(("grp", "dev"), None, None)
    return jax.shard_map(
        per_device,
        mesh=mesh,
        in_specs=(rows2, rows2) + (rows3,) * 6,
        out_specs=(rows2, rows2),
        check_vma=False,
    )
```

time: 59.6 us -> 62 us (1.040)
  starting transfers between devices: 20.1 us -> 24.3 us
  waiting for transfers between devices: 29.2 us -> 25.2 us
  Pallas kernels: 8.29 us -> 9.56 us
  local copies, waits for them, and re-layouts: 0.18 us -> 0.85 us
    ppermute x16 -> x21, starting transfers between devices: 20.1 us -> 24.3 us  [swap(): return lax.ppermute(value, axis, [(i, i ^ bit) for i in range(size)])]
    ppermute x16 -> x21, waiting for transfers between devices: 29.2 us -> 25.2 us  [swap(): return lax.ppermute(value, axis, [(i, i ^ bit) for i in range(size)])]
    pallas_call x2 -> x9, Pallas kernels: 8.29 us -> 9.56 us  [the longest x8 8.81 us: call(): pl.pallas_call(functools.partial(kernel, [m for _, m in pieces], axis, ro...]
    unnamed x0 -> x1, other arithmetic: none -> 0.85 us
    convert_element_type x1 -> x0, other arithmetic: 0.85 us -> none  [per_device(): packed = item_factors.astype(jnp.bfloat16)]
    unnamed x22 -> x25, local copies, waits for them, and re-layouts: 0.1 us -> 0.76 us
  transfers between devices with their start and end apart: 16 -> 21, of which waited for: 11 -> 10; matrix products, arithmetic and copies ran while one was open for 0% -> 0% of each run, Pallas kernels for 0% -> 8%
where the time goes in v3:
time: 62 us; the launch traced here: 61.7 us
  waiting for transfers between devices  25.2 us (41%)
  starting transfers between devices  24.3 us (39%)
  Pallas kernels  9.56 us (15%)
  other arithmetic  0.88 us (1%)
  between operations  0.87 us (1%)
  local copies, waits for them, and re-layouts  0.85 us (1%)
    ppermute x21, waiting for transfers between devices, swap(): return lax.ppermute(value, axis, [(i, i ^ bit) for i in range(size)])  25.2 us
    ppermute x21, starting transfers between devices, swap(): return lax.ppermute(value, axis, [(i, i ^ bit) for i in range(size)])  24.3 us
    pallas_call x8, Pallas kernels, call(): pl.pallas_call(functools.partial(kernel, [m for _, m in pieces], axis, ro...  8.81 us
  transfers between devices with their start and end apart: 21, of which 10 were waited for; matrix products, arithmetic and copies ran while one was open for 0% of the time, Pallas kernels for 8%

profile of v3, /device:TPU:0, one launch (start us, length us, event | category | flops | bytes accessed | tf_op | source)
XLA Modules:
  0.0 61.7 jit_solution(14931485460033805560)
XLA Ops:
  0.6 0.8 %constant_dynamic-update-slice_fusion.5 = (bf16[640,256]{1,0:T(8,128)(2,1)S(1)}, bf16[64,256]{1,0:T(8,128)(2,1)S(1)}) fusion(f32[64,256]{1,0:T(8,128)} %refs_3_.3), kind=kLoop, calls=%fused_computation.8 | loop fusion | flops 16383 | bytes 131072
  1.5 4.1 %collective-permute-start = (bf16[64,256]{1,0:T(8,128)(2,1)S(1)}, bf16[64,256]{1,0:T(8,128)(2,1)S(1)}, u32[]{:S(2)}, u32[]{:S(2)}) collective-permute-start(bf16[64,256]{1,0:T(8,128)(2,1)S(1)} %get-tuple-element.45), channel_id=1, source_target_pairs={{0,8},{1,9},{2,10},{3,11},{4,12},{5,13},{6,14},{7,15},{8,0},{9,1},... | collective-permute-start | bytes 98312 | tf_op jit(solution)/shard_map/ppermute | solution.py:20
  5.5 2.2 %collective-permute-done = bf16[64,256]{1,0:T(8,128)(2,1)S(1)} collective-permute-done((bf16[64,256]{1,0:T(8,128)(2,1)S(1)}, bf16[64,256]{1,0:T(8,128)(2,1)S(1)}, u32[]{:S(2)}, u32[]{:S(2)}) %collective-permute-start) | collective-permute-done | bytes 32800 | tf_op jit(solution)/shard_map/ppermute | solution.py:20
  7.8 1.6 %collective-permute-start.1 = (bf16[128,256]{1,0:T(8,128)(2,1)S(1)}, bf16[128,256]{1,0:T(8,128)(2,1)S(1)}, u32[]{:S(2)}, u32[]{:S(2)}) collective-permute-start(bf16[128,256]{1,0:T(8,128)(2,1)S(1)} %pad_maximum_fusion.2), channel_id=1, source_target_pairs={{0,4},{1,5},{2,6},{3,7},{4,0},{5,1},{6,2},{7,3},{8,12},{9,13},{10,... | collective-permute-start | bytes 196616 | tf_op jit(solution)/shard_map/ppermute | solution.py:20
  9.4 1.5 %collective-permute-start.2 = (bf16[128,256]{1,0:T(8,128)(2,1)S(1)}, bf16[128,256]{1,0:T(8,128)(2,1)S(1)}, u32[]{:S(2)}, u32[]{:S(2)}) collective-permute-start(bf16[128,256]{1,0:T(8,128)(2,1)S(1)} %pad_maximum_fusion.2), channel_id=1, source_target_pairs={{0,1},{1,0},{2,3},{3,2},{4,5},{5,4},{6,7},{7,6},{8,9},{9,8},{10,11... | collective-permute-start | bytes 196616 | tf_op jit(solution)/shard_map/ppermute | solution.py:20
  10.8 1.5 %collective-permute-start.3 = (bf16[128,256]{1,0:T(8,128)(2,1)S(1)}, bf16[128,256]{1,0:T(8,128)(2,1)S(1)}, u32[]{:S(2)}, u32[]{:S(2)}) collective-permute-start(bf16[128,256]{1,0:T(8,128)(2,1)S(1)} %pad_maximum_fusion.2), channel_id=1, source_target_pairs={{0,2},{1,3},{2,0},{3,1},{4,6},{5,7},{6,4},{7,5},{8,10},{9,11},{10,... | collective-permute-start | bytes 196616 | tf_op jit(solution)/shard_map/ppermute | solution.py:20
  12.4 0.0 collective-permute-done.1
  12.4 1.2 %collective-permute-done.2 = bf16[128,256]{1,0:T(8,128)(2,1)S(1)} collective-permute-done((bf16[128,256]{1,0:T(8,128)(2,1)S(1)}, bf16[128,256]{1,0:T(8,128)(2,1)S(1)}, u32[]{:S(2)}, u32[]{:S(2)}) %collective-permute-start.2) | collective-permute-done | bytes 65568 | tf_op jit(solution)/shard_map/ppermute | solution.py:20
  13.6 1.6 %collective-permute-start.6 = (bf16[256,256]{1,0:T(8,128)(2,1)S(1)}, bf16[256,256]{1,0:T(8,128)(2,1)S(1)}, u32[]{:S(2)}, u32[]{:S(2)}) collective-permute-start(bf16[256,256]{1,0:T(8,128)(2,1)S(1)} %pad_maximum_fusion.1), channel_id=1, source_target_pairs={{0,2},{1,3},{2,0},{3,1},{4,6},{5,7},{6,4},{7,5},{8,10},{9,11},{10,... | collective-permute-start | bytes 393224 | tf_op jit(solution)/shard_map/ppermute | solution.py:20
  15.2 1.5 %collective-permute-start.4 = (bf16[128,256]{1,0:T(8,128)(2,1)S(1)}, bf16[128,256]{1,0:T(8,128)(2,1)S(1)}, u32[]{:S(2)}, u32[]{:S(2)}) collective-permute-start(bf16[128,256]{1,0:T(8,128)(2,1)S(1)} %collective-permute-done.1), channel_id=1, source_target_pairs={{0,1},{1,0},{2,3},{3,2},{4,5},{5,4},{6,7},{7,6},{8,9},{9,8},{10,11... | collective-permute-start | bytes 196616 | tf_op jit(solution)/shard_map/ppermute | solution.py:20
  16.7 0.0 collective-permute-done.3
  16.7 2.7 %collective-permute-done.4 = bf16[128,256]{1,0:T(8,128)(2,1)S(1)} collective-permute-done((bf16[128,256]{1,0:T(8,128)(2,1)S(1)}, bf16[128,256]{1,0:T(8,128)(2,1)S(1)}, u32[]{:S(2)}, u32[]{:S(2)}) %collective-permute-start.4) | collective-permute-done | bytes 65568 | tf_op jit(solution)/shard_map/ppermute | solution.py:20
  19.5 0.0 copy-start.3
  19.5 0.1 collective-permute-start.5
  19.6 0.6 collective-permute-start.7
  20.1 0.0 collective-permute-done.6.refs_3_
  20.1 3.9 %collective-permute-done.7.refs_3_ = bf16[128,256]{1,0:T(8,128)(2,1)S(1)} collective-permute-done((bf16[128,256]{1,0:T(8,128)(2,1)S(1)}, bf16[128,256]{1,0:T(8,128)(2,1)S(1)}, u32[]{:S(2)}, u32[]{:S(2)}) %collective-permute-start.7) | collective-permute-done | bytes 65568 | tf_op jit(solution)/shard_map/ppermute | solution.py:20
  24.1 0.0 copy-start.6
  24.1 0.0 copy-start.1
  24.1 0.1 collective-permute-start.8
  24.2 0.0 collective-permute-done.5.refs_5_
  24.2 0.0 copy-done.3
  24.2 0.6 copy-done.6
  24.8 0.0 copy-done.7
  24.8 0.0 copy-done.1
  24.8 0.9 %shard_map.95 = (f32[256,256]{1,0:T(8,128)S(1)}, f32[6,256,128]{2,1,0:T(8,128)S(1)}, f32[256,128]{1,0:T(8,128)S(1)}, f32[6,128]{1,0:T(8,128)S(1)}, f32[6,128]{1,0:T(8,128)S(1)}) custom-call(s32[3,2,128]{2,1,0:T(2,128)S(1)} %bitcast.6, f32[3,2,128]{2,1,0:T(2,128)S(1)} %bitcast.16, s32[3,2,128]{2,1,0:T(2,128)S(1)} %bitcast.17, f32[128,256]{1,0:T(8,128)S(1)} %copy-done.3, ...), custom_call_target="tpu_custom_call" | custom-call | flops 419430400 | bytes 655360 | tf_op jit(solution)/shard_map/pallas_call | solution.py:237
  25.7 0.3 shard_map.96
  26.0 0.3 shard_map.97
  26.3 0.0 collective-permute-done.8.refs_6_
  26.3 2.0 %shard_map.98 = (f32[256,128]{1,0:T(8,128)S(1)}, bf16[256,128]{1,0:T(8,128)(2,1)S(1)}) custom-call(s32[3,2,128]{2,1,0:T(2,128)S(1)} %bitcast.9, f32[256,256]{1,0:T(8,128)S(1)} %get-tuple-element.27.refs_1_, f32[6,256,128]{2,1,0:T(8,128)S(1)} %get-tuple-element.28.refs_2_, f32[256,128]{1,0:T(8,128)S(1)} %get-tuple-element.29.refs_3_, ...), custom_call_target="tpu_custom_call" | custom-call | flops 125829120 | bytes 196608 | tf_op jit(solution)/shard_map/pallas_call | solution.py:237
  28.3 0.8 %collective-permute-start.10 = (bf16[256,128]{1,0:T(8,128)(2,1)S(1)}, bf16[256,128]{1,0:T(8,128)(2,1)S(1)}, u32[]{:S(2)}, u32[]{:S(2)}) collective-permute-start(bf16[256,128]{1,0:T(8,128)(2,1)S(1)} %get-tuple-element.33), channel_id=1, source_target_pairs={{0,4},{1,5},{2,6},{3,7},{4,0},{5,1},{6,2},{7,3},{8,12},{9,13},{10,... | collective-permute-start | bytes 196616 | tf_op jit(solution)/shard_map/ppermute | solution.py:20
  29.1 2.3 %collective-permute-start.9 = (bf16[256,128]{1,0:T(8,128)(2,1)S(1)}, bf16[256,128]{1,0:T(8,128)(2,1)S(1)}, u32[]{:S(2)}, u32[]{:S(2)}) collective-permute-start(bf16[256,128]{1,0:T(8,128)(2,1)S(1)} %get-tuple-element.33), channel_id=1, source_target_pairs={{0,8},{1,9},{2,10},{3,11},{4,12},{5,13},{6,14},{7,15},{8,0},{9,1},... | collective-permute-start | bytes 196616 | tf_op jit(solution)/shard_map/ppermute | solution.py:20
  31.4 3.5 %collective-permute-done.9 = bf16[256,128]{1,0:T(8,128)(2,1)S(1)} collective-permute-done((bf16[256,128]{1,0:T(8,128)(2,1)S(1)}, bf16[256,128]{1,0:T(8,128)(2,1)S(1)}, u32[]{:S(2)}, u32[]{:S(2)}) %collective-permute-start.9) | collective-permute-done | bytes 65568 | tf_op jit(solution)/shard_map/ppermute | solution.py:20
  35.0 1.6 %collective-permute-start.12 = (bf16[256,256]{1,0:T(8,128)(2,1)S(1)}, bf16[256,256]{1,0:T(8,128)(2,1)S(1)}, u32[]{:S(2)}, u32[]{:S(2)}) collective-permute-start(bf16[256,256]{1,0:T(8,128)(2,1)S(1)} %get-tuple-element.50), channel_id=1, source_target_pairs={{0,1},{1,0},{2,3},{3,2},{4,5},{5,4},{6,7},{7,6},{8,9},{9,8},{10,11... | collective-permute-start | bytes 393224 | tf_op jit(solution)/shard_map/ppermute | solution.py:20
  36.6 0.4 collective-permute-start.13
  37.0 1.6 %collective-permute-start.11 = (bf16[256,128]{1,0:T(8,128)(2,1)S(1)}, bf16[256,128]{1,0:T(8,128)(2,1)S(1)}, u32[]{:S(2)}, u32[]{:S(2)}) collective-permute-start(bf16[256,128]{1,0:T(8,128)(2,1)S(1)} %collective-permute-done.9), channel_id=1, source_target_pairs={{0,4},{1,5},{2,6},{3,7},{4,0},{5,1},{6,2},{7,3},{8,12},{9,13},{10,... | collective-permute-start | bytes 196616 | tf_op jit(solution)/shard_map/ppermute | solution.py:20
  38.6 0.0 collective-permute-done.10
  38.6 2.6 %collective-permute-done.11 = bf16[256,128]{1,0:T(8,128)(2,1)S(1)} collective-permute-done((bf16[256,128]{1,0:T(8,128)(2,1)S(1)}, bf16[256,128]{1,0:T(8,128)(2,1)S(1)}, u32[]{:S(2)}, u32[]{:S(2)}) %collective-permute-start.11) | collective-permute-done | bytes 65568 | tf_op jit(solution)/shard_map/ppermute | solution.py:20
  41.3 0.3 collective-permute-start.15
  41.6 1.9 %collective-permute-start.16 = (bf16[256,256]{1,0:T(8,128)(2,1)S(1)}, bf16[256,256]{1,0:T(8,128)(2,1)S(1)}, u32[]{:S(2)}, u32[]{:S(2)}) collective-permute-start(bf16[256,256]{1,0:T(8,128)(2,1)S(1)} %get-tuple-element.46), channel_id=1, source_target_pairs={{0,2},{1,3},{2,0},{3,1},{4,6},{5,7},{6,4},{7,5},{8,10},{9,11},{10,... | collective-permute-start | bytes 393224 | tf_op jit(solution)/shard_map/ppermute | solution.py:20
  43.5 0.0 collective-permute-done.12
  43.5 0.0 collective-permute-done.13
  43.5 0.1 collective-permute-start.14
  43.6 1.6 %collective-permute-start.17 = (bf16[256,256]{1,0:T(8,128)(2,1)S(1)}, bf16[256,256]{1,0:T(8,128)(2,1)S(1)}, u32[]{:S(2)}, u32[]{:S(2)}) collective-permute-start(bf16[256,256]{1,0:T(8,128)(2,1)S(1)} %collective-permute-done.13), channel_id=1, source_target_pairs={{0,1},{1,0},{2,3},{3,2},{4,5},{5,4},{6,7},{7,6},{8,9},{9,8},{10,11... | collective-permute-start | bytes 393224 | tf_op jit(solution)/shard_map/ppermute | solution.py:20
  45.2 1.2 %collective-permute-done.15 = bf16[256,256]{1,0:T(8,128)(2,1)S(1)} collective-permute-done((bf16[256,256]{1,0:T(8,128)(2,1)S(1)}, bf16[256,256]{1,0:T(8,128)(2,1)S(1)}, u32[]{:S(2)}, u32[]{:S(2)}) %collective-permute-start.15) | collective-permute-done | bytes 131104 | tf_op jit(solution)/shard_map/ppermute | solution.py:20
  46.4 0.2 collective-permute-done.16
  46.6 3.0 %collective-permute-done.17 = bf16[256,256]{1,0:T(8,128)(2,1)S(1)} collective-permute-done((bf16[256,256]{1,0:T(8,128)(2,1)S(1)}, bf16[256,256]{1,0:T(8,128)(2,1)S(1)}, u32[]{:S(2)}, u32[]{:S(2)}) %collective-permute-start.17) | collective-permute-done | bytes 131104 | tf_op jit(solution)/shard_map/ppermute | solution.py:20
  49.5 0.1 collective-permute-start.18
  49.6 1.3 %collective-permute-start.19 = (bf16[256,256]{1,0:T(8,128)(2,1)S(1)}, bf16[256,256]{1,0:T(8,128)(2,1)S(1)}, u32[]{:S(2)}, u32[]{:S(2)}) collective-permute-start(bf16[256,256]{1,0:T(8,128)(2,1)S(1)} %collective-permute-done.15), channel_id=1, source_target_pairs={{0,2},{1,3},{2,0},{3,1},{4,6},{5,7},{6,4},{7,5},{8,10},{9,11},{10,... | collective-permute-start | bytes 393224 | tf_op jit(solution)/shard_map/ppermute | solution.py:20
  50.9 4.6 %collective-permute-done.19.refs_3_ = bf16[256,256]{1,0:T(8,128)(2,1)S(1)} collective-permute-done((bf16[256,256]{1,0:T(8,128)(2,1)S(1)}, bf16[256,256]{1,0:T(8,128)(2,1)S(1)}, u32[]{:S(2)}, u32[]{:S(2)}) %collective-permute-start.19) | collective-permute-done | bytes 131104 | tf_op jit(solution)/shard_map/ppermute | solution.py:20
  55.5 0.0 collective-permute-start.20
  55.5 0.0 copy-start.5
  55.5 0.8 %turn.1 = f32[128,256]{1,0:T(8,128)} custom-call(f32[256,128]{1,0:T(8,128)S(1)} %get-tuple-element.32.value_ref), custom_call_target="tpu_custom_call" | custom-call | tf_op jit(solution)/shard_map/turn/pallas_call | solution.py:286
  56.3 0.0 collective-permute-done.14.refs_5_
  56.3 0.1 copy-done
  56.4 0.0 copy-done.2
  56.4 0.0 copy-done.4
  56.4 0.0 copy-done.5
  56.4 1.1 %shard_map.99 = (f32[256,256]{1,0:T(8,128)S(1)}, f32[6,256,128]{2,1,0:T(8,128)S(1)}, f32[256,128]{1,0:T(8,128)S(1)}, f32[6,128]{1,0:T(8,128)S(1)}, f32[6,128]{1,0:T(8,128)S(1)}) custom-call(s32[6,2,64]{2,1,0:T(2,128)S(1)} %bitcast.10, f32[6,2,64]{2,1,0:T(2,128)S(1)} %bitcast.14, s32[6,2,64]{2,1,0:T(2,128)S(1)} %bitcast.15, f32[64,256]{1,0:T(8,128)S(1)} %copy-done, ...), custom_call_target="tpu_custom_call" | custom-call | flops 671088640 | bytes 1048576 | tf_op jit(solution)/shard_map/pallas_call | solution.py:237
  57.5 0.0 collective-permute-done.18.refs_4_
  57.5 0.9 %shard_map.100 = (f32[256,256]{1,0:T(8,128)S(1)}, f32[6,256,128]{2,1,0:T(8,128)S(1)}) custom-call(s32[6,2,64]{2,1,0:T(2,128)S(1)} %bitcast.11, f32[256,256]{1,0:T(8,128)S(1)} %get-tuple-element.34.refs_1_, f32[6,256,128]{2,1,0:T(8,128)S(1)} %get-tuple-element.35.refs_2_, bf16[256,768]{1,0:T(8,128)(2,1)S(1)} %constant_dynamic-update-slice_fusion.16.refs_3_, ...), custom_call_target="tpu_custom_call" | custom-call | flops 503316480 | bytes 786432 | tf_op jit(solution)/shard_map/pallas_call | solution.py:237
  58.5 0.4 shard_map.101
  58.8 0.0 collective-permute-done.20.refs_6_
  58.8 2.9 %shard_map.102 = (f32[64,256]{1,0:T(8,128)}, bf16[256,64]{1,0:T(8,128)(2,1)}) custom-call(s32[6,2,64]{2,1,0:T(2,128)S(1)} %bitcast.13, f32[256,256]{1,0:T(8,128)S(1)} %get-tuple-element.38.refs_1_, f32[6,256,128]{2,1,0:T(8,128)S(1)} %get-tuple-element.39.refs_2_, f32[256,128]{1,0:T(8,128)S(1)} %get-tuple-element.40.refs_3_, ...), custom_call_target="tpu_custom_call" | custom-call | flops 83886080 | bytes 131072 | tf_op jit(solution)/shard_map/pallas_call | solution.py:237
  (21 shorter events, 0.2 us)
Async XLA Ops:
  1.5 6.3 %collective-permute-start = (bf16[64,256]{1,0:T(8,128)(2,1)S(1)}, bf16[64,256]{1,0:T(8,128)(2,1)S(1)}, u32[]{:S(2)}, u32[]{:S(2)}) collective-permute-start(bf16[64,256]{1,0:T(8,128)(2,1)S(1)} %get-tuple-element.45), channel_id=1, source_target_pairs={{0,8},{1,9},{2,10},{3,11},{4,12},{5,13},{6,14},{7,15},{8,0},{9,1},... | collective-permute-start | bytes 98312 | tf_op jit(solution)/shard_map/ppermute | solution.py:20
  7.8 4.6 %collective-permute-start.1 = (bf16[128,256]{1,0:T(8,128)(2,1)S(1)}, bf16[128,256]{1,0:T(8,128)(2,1)S(1)}, u32[]{:S(2)}, u32[]{:S(2)}) collective-permute-start(bf16[128,256]{1,0:T(8,128)(2,1)S(1)} %pad_maximum_fusion.2), channel_id=1, source_target_pairs={{0,4},{1,5},{2,6},{3,7},{4,0},{5,1},{6,2},{7,3},{8,12},{9,13},{10,... | collective-permute-start | bytes 196616 | tf_op jit(solution)/shard_map/ppermute | solution.py:20
  9.4 4.3 %collective-permute-start.2 = (bf16[128,256]{1,0:T(8,128)(2,1)S(1)}, bf16[128,256]{1,0:T(8,128)(2,1)S(1)}, u32[]{:S(2)}, u32[]{:S(2)}) collective-permute-start(bf16[128,256]{1,0:T(8,128)(2,1)S(1)} %pad_maximum_fusion.2), channel_id=1, source_target_pairs={{0,1},{1,0},{2,3},{3,2},{4,5},{5,4},{6,7},{7,6},{8,9},{9,8},{10,11... | collective-permute-start | bytes 196616 | tf_op jit(solution)/shard_map/ppermute | solution.py:20
  10.8 5.9 %collective-permute-start.3 = (bf16[128,256]{1,0:T(8,128)(2,1)S(1)}, bf16[128,256]{1,0:T(8,128)(2,1)S(1)}, u32[]{:S(2)}, u32[]{:S(2)}) collective-permute-start(bf16[128,256]{1,0:T(8,128)(2,1)S(1)} %pad_maximum_fusion.2), channel_id=1, source_target_pairs={{0,2},{1,3},{2,0},{3,1},{4,6},{5,7},{6,4},{7,5},{8,10},{9,11},{10,... | collective-permute-start | bytes 196616 | tf_op jit(solution)/shard_map/ppermute | solution.py:20
  13.6 6.5 %collective-permute-start.6 = (bf16[256,256]{1,0:T(8,128)(2,1)S(1)}, bf16[256,256]{1,0:T(8,128)(2,1)S(1)}, u32[]{:S(2)}, u32[]{:S(2)}) collective-permute-start(bf16[256,256]{1,0:T(8,128)(2,1)S(1)} %pad_maximum_fusion.1), channel_id=1, source_target_pairs={{0,2},{1,3},{2,0},{3,1},{4,6},{5,7},{6,4},{7,5},{8,10},{9,11},{10,... | collective-permute-start | bytes 393224 | tf_op jit(solution)/shard_map/ppermute | solution.py:20
  15.2 4.3 %collective-permute-start.4 = (bf16[128,256]{1,0:T(8,128)(2,1)S(1)}, bf16[128,256]{1,0:T(8,128)(2,1)S(1)}, u32[]{:S(2)}, u32[]{:S(2)}) collective-permute-start(bf16[128,256]{1,0:T(8,128)(2,1)S(1)} %collective-permute-done.1), channel_id=1, source_target_pairs={{0,1},{1,0},{2,3},{3,2},{4,5},{5,4},{6,7},{7,6},{8,9},{9,8},{10,11... | collective-permute-start | bytes 196616 | tf_op jit(solution)/shard_map/ppermute | solution.py:20
  19.5 4.7 %copy-start.3 = (f32[128,256]{1,0:T(8,128)S(1)}, f32[128,256]{1,0:T(8,128)}, u32[]{:S(2)}) copy-start(f32[128,256]{1,0:T(8,128)} %refs_3_.2) | copy-start | bytes 393220
  19.5 4.7 %collective-permute-start.5 = (bf16[640,256]{1,0:T(8,128)(2,1)S(1)}, bf16[640,256]{1,0:T(8,128)(2,1)S(1)}, u32[]{:S(2)}, u32[]{:S(2)}) collective-permute-start(bf16[640,256]{1,0:T(8,128)(2,1)S(1)} %constant_dynamic-update-slice_fusion.refs_4_), channel_id=1, source_target_pairs={{0,16},{16,0},{1,17},{17,1},{2,18},{18,2},{3,19},{19,3},{4,20},{20... | collective-permute-start | bytes 983048 | tf_op jit(solution)/shard_map/ppermute | solution.py:20
  19.6 4.5 %collective-permute-start.7 = (bf16[128,256]{1,0:T(8,128)(2,1)S(1)}, bf16[128,256]{1,0:T(8,128)(2,1)S(1)}, u32[]{:S(2)}, u32[]{:S(2)}) collective-permute-start(bf16[128,256]{1,0:T(8,128)(2,1)S(1)} %collective-permute-done.4), channel_id=1, source_target_pairs={{0,2},{1,3},{2,0},{3,1},{4,6},{5,7},{6,4},{7,5},{8,10},{9,11},{10,... | collective-permute-start | bytes 196616 | tf_op jit(solution)/shard_map/ppermute | solution.py:20
  24.1 0.7 %copy-start.6 = (f32[128,2,3]{0,1,2:T(2,128)S(1)}, f32[128,2,3]{0,1,2:T(2,128)}, u32[]{:S(2)}) copy-start(f32[128,2,3]{0,1,2:T(2,128)} %param.11) | copy-start | bytes 9220
  24.1 0.7 %copy-start.7 = (s32[128,2,3]{0,1,2:T(2,128)S(1)}, s32[128,2,3]{0,1,2:T(2,128)}, u32[]{:S(2)}) copy-start(s32[128,2,3]{0,1,2:T(2,128)} %param.12) | copy-start | bytes 9220
  24.1 0.7 %copy-start.1 = (s32[128,2,3]{0,1,2:T(2,128)S(1)}, s32[128,2,3]{0,1,2:T(2,128)}, u32[]{:S(2)}) copy-start(s32[128,2,3]{0,1,2:T(2,128)} %param.10) | copy-start | bytes 9220
  24.1 2.2 %collective-permute-start.8 = (bf16[384,256]{1,0:T(8,128)(2,1)S(1)}, bf16[384,256]{1,0:T(8,128)(2,1)S(1)}, u32[]{:S(2)}, u32[]{:S(2)}) collective-permute-start(bf16[384,256]{1,0:T(8,128)(2,1)S(1)} %pad_maximum_fusion), channel_id=1, source_target_pairs={{0,16},{16,0},{1,17},{17,1},{2,18},{18,2},{3,19},{19,3},{4,20},{20... | collective-permute-start | bytes 589832 | tf_op jit(solution)/shard_map/ppermute | solution.py:20
  28.3 10.3 %collective-permute-start.10 = (bf16[256,128]{1,0:T(8,128)(2,1)S(1)}, bf16[256,128]{1,0:T(8,128)(2,1)S(1)}, u32[]{:S(2)}, u32[]{:S(2)}) collective-permute-start(bf16[256,128]{1,0:T(8,128)(2,1)S(1)} %get-tuple-element.33), channel_id=1, source_target_pairs={{0,4},{1,5},{2,6},{3,7},{4,0},{5,1},{6,2},{7,3},{8,12},{9,13},{10,... | collective-permute-start | bytes 196616 | tf_op jit(solution)/shard_map/ppermute | solution.py:20
  29.1 5.9 %collective-permute-start.9 = (bf16[256,128]{1,0:T(8,128)(2,1)S(1)}, bf16[256,128]{1,0:T(8,128)(2,1)S(1)}, u32[]{:S(2)}, u32[]{:S(2)}) collective-permute-start(bf16[256,128]{1,0:T(8,128)(2,1)S(1)} %get-tuple-element.33), channel_id=1, source_target_pairs={{0,8},{1,9},{2,10},{3,11},{4,12},{5,13},{6,14},{7,15},{8,0},{9,1},... | collective-permute-start | bytes 196616 | tf_op jit(solution)/shard_map/ppermute | solution.py:20
  35.0 8.5 %collective-permute-start.12 = (bf16[256,256]{1,0:T(8,128)(2,1)S(1)}, bf16[256,256]{1,0:T(8,128)(2,1)S(1)}, u32[]{:S(2)}, u32[]{:S(2)}) collective-permute-start(bf16[256,256]{1,0:T(8,128)(2,1)S(1)} %get-tuple-element.50), channel_id=1, source_target_pairs={{0,1},{1,0},{2,3},{3,2},{4,5},{5,4},{6,7},{7,6},{8,9},{9,8},{10,11... | collective-permute-start | bytes 393224 | tf_op jit(solution)/shard_map/ppermute | solution.py:20
  36.6 6.9 %collective-permute-start.13 = (bf16[256,256]{1,0:T(8,128)(2,1)S(1)}, bf16[256,256]{1,0:T(8,128)(2,1)S(1)}, u32[]{:S(2)}, u32[]{:S(2)}) collective-permute-start(bf16[256,256]{1,0:T(8,128)(2,1)S(1)} %get-tuple-element.50), channel_id=1, source_target_pairs={{0,2},{1,3},{2,0},{3,1},{4,6},{5,7},{6,4},{7,5},{8,10},{9,11},{10,... | collective-permute-start | bytes 393224 | tf_op jit(solution)/shard_map/ppermute | solution.py:20
  37.0 4.3 %collective-permute-start.11 = (bf16[256,128]{1,0:T(8,128)(2,1)S(1)}, bf16[256,128]{1,0:T(8,128)(2,1)S(1)}, u32[]{:S(2)}, u32[]{:S(2)}) collective-permute-start(bf16[256,128]{1,0:T(8,128)(2,1)S(1)} %collective-permute-done.9), channel_id=1, source_target_pairs={{0,4},{1,5},{2,6},{3,7},{4,0},{5,1},{6,2},{7,3},{8,12},{9,13},{10,... | collective-permute-start | bytes 196616 | tf_op jit(solution)/shard_map/ppermute | solution.py:20
  41.3 5.0 %collective-permute-start.15 = (bf16[256,256]{1,0:T(8,128)(2,1)S(1)}, bf16[256,256]{1,0:T(8,128)(2,1)S(1)}, u32[]{:S(2)}, u32[]{:S(2)}) collective-permute-start(bf16[256,256]{1,0:T(8,128)(2,1)S(1)} %get-tuple-element.46), channel_id=1, source_target_pairs={{0,1},{1,0},{2,3},{3,2},{4,5},{5,4},{6,7},{7,6},{8,9},{9,8},{10,11... | collective-permute-start | bytes 393224 | tf_op jit(solution)/shard_map/ppermute | solution.py:20
  41.6 5.0 %collective-permute-start.16 = (bf16[256,256]{1,0:T(8,128)(2,1)S(1)}, bf16[256,256]{1,0:T(8,128)(2,1)S(1)}, u32[]{:S(2)}, u32[]{:S(2)}) collective-permute-start(bf16[256,256]{1,0:T(8,128)(2,1)S(1)} %get-tuple-element.46), channel_id=1, source_target_pairs={{0,2},{1,3},{2,0},{3,1},{4,6},{5,7},{6,4},{7,5},{8,10},{9,11},{10,... | collective-permute-start | bytes 393224 | tf_op jit(solution)/shard_map/ppermute | solution.py:20
  43.5 12.8 %collective-permute-start.14 = (bf16[256,1024]{1,0:T(8,128)(2,1)S(1)}, bf16[256,1024]{1,0:T(8,128)(2,1)S(1)}, u32[]{:S(2)}, u32[]{:S(2)}) collective-permute-start(bf16[256,1024]{1,0:T(8,128)(2,1)S(1)} %constant_dynamic-update-slice_fusion.8.refs_4_), channel_id=1, source_target_pairs={{0,16},{16,0},{1,17},{17,1},{2,18},{18,2},{3,19},{19,3},{4,20},{20... | collective-permute-start | bytes 1572872 | tf_op jit(solution)/shard_map/ppermute | solution.py:20
  43.6 5.9 %collective-permute-start.17 = (bf16[256,256]{1,0:T(8,128)(2,1)S(1)}, bf16[256,256]{1,0:T(8,128)(2,1)S(1)}, u32[]{:S(2)}, u32[]{:S(2)}) collective-permute-start(bf16[256,256]{1,0:T(8,128)(2,1)S(1)} %collective-permute-done.13), channel_id=1, source_target_pairs={{0,1},{1,0},{2,3},{3,2},{4,5},{5,4},{6,7},{7,6},{8,9},{9,8},{10,11... | collective-permute-start | bytes 393224 | tf_op jit(solution)/shard_map/ppermute | solution.py:20
  49.5 8.0 %collective-permute-start.18 = (bf16[256,768]{1,0:T(8,128)(2,1)S(1)}, bf16[256,768]{1,0:T(8,128)(2,1)S(1)}, u32[]{:S(2)}, u32[]{:S(2)}) collective-permute-start(bf16[256,768]{1,0:T(8,128)(2,1)S(1)} %constant_dynamic-update-slice_fusion.16.refs_3_), channel_id=1, source_target_pairs={{0,16},{16,0},{1,17},{17,1},{2,18},{18,2},{3,19},{19,3},{4,20},{20... | collective-permute-start | bytes 1179656 | tf_op jit(solution)/shard_map/ppermute | solution.py:20
  49.6 5.9 %collective-permute-start.19 = (bf16[256,256]{1,0:T(8,128)(2,1)S(1)}, bf16[256,256]{1,0:T(8,128)(2,1)S(1)}, u32[]{:S(2)}, u32[]{:S(2)}) collective-permute-start(bf16[256,256]{1,0:T(8,128)(2,1)S(1)} %collective-permute-done.15), channel_id=1, source_target_pairs={{0,2},{1,3},{2,0},{3,1},{4,6},{5,7},{6,4},{7,5},{8,10},{9,11},{10,... | collective-permute-start | bytes 393224 | tf_op jit(solution)/shard_map/ppermute | solution.py:20
  55.5 3.3 %collective-permute-start.20 = (bf16[256,256]{1,0:T(8,128)(2,1)S(1)}, bf16[256,256]{1,0:T(8,128)(2,1)S(1)}, u32[]{:S(2)}, u32[]{:S(2)}) collective-permute-start(bf16[256,256]{1,0:T(8,128)(2,1)S(1)} %collective-permute-done.19.refs_3_), channel_id=1, source_target_pairs={{0,16},{16,0},{1,17},{17,1},{2,18},{18,2},{3,19},{19,3},{4,20},{20... | collective-permute-start | bytes 393224 | tf_op jit(solution)/shard_map/ppermute | solution.py:20
  55.5 0.8 %copy-start = (f32[64,256]{1,0:T(8,128)S(1)}, f32[64,256]{1,0:T(8,128)}, u32[]{:S(2)}) copy-start(f32[64,256]{1,0:T(8,128)} %refs_3_.3) | copy-start | bytes 196612
  55.5 0.8 %copy-start.2 = (s32[64,2,6]{0,1,2:T(2,128)S(1)}, s32[64,2,6]{0,1,2:T(2,128)}, u32[]{:S(2)}) copy-start(s32[64,2,6]{0,1,2:T(2,128)} %param.13) | copy-start | bytes 9220
  55.5 0.8 %copy-start.4 = (f32[64,2,6]{0,1,2:T(2,128)S(1)}, f32[64,2,6]{0,1,2:T(2,128)}, u32[]{:S(2)}) copy-start(f32[64,2,6]{0,1,2:T(2,128)} %param.14) | copy-start | bytes 9220
  55.5 0.8 %copy-start.5 = (s32[64,2,6]{0,1,2:T(2,128)S(1)}, s32[64,2,6]{0,1,2:T(2,128)}, u32[]{:S(2)}) copy-start(s32[64,2,6]{0,1,2:T(2,128)} %param.15) | copy-start | bytes 9220
